TPU v7x, 32 devices: a whole 2x2x4 slice. The times are simulated.
32 devices in a mesh: ep: 32 (over z, y, x, core).
Axes of the slice: x: 2, y: 2, z: 4, core: 2. Of those that a mesh axis runs over, the one named last changes fastest.
Arguments:
- x: bfloat16 [32768, 768], P('ep')
- gate_w: bfloat16 [768, 64], replicated
- up_w: bfloat16 [64, 768, 3072], P('ep')
- down_w: bfloat16 [64, 3072, 768], P('ep')
- expert_picks: int32 [64, 1024], P('ep')
- loss_w: bfloat16 [32768, 768], P('ep')
Outputs:
- output 1: bfloat16 [32768, 768], P('ep')
- output 2: float32 [], replicated
- output 3: bfloat16 [32768, 768], P('ep')
- output 4: bfloat16 [64, 768, 3072], P('ep')
- output 5: bfloat16 [64, 3072, 768], P('ep')
- output 6: float32 [768, 64], replicated
All inputs are finite; a program needn't handle non-finite values.
Results may differ from a plain program's by a relative error of at most 0.0107156.
Values are sent between devices in bfloat16 or wider.
A program may use at most 1 GiB of HBM per device.

v0:
```python
import math
import jax
import jax.numpy as jnp
from jax import lax
from jax.sharding import PartitionSpec as P


def solution(mesh):
    group_size = mesh.shape['ep']

    def device_step(x, gate_w, up_w, down_w, expert_picks, loss_w):
        tok_dev, hidden = x.shape
        local_experts, capacity = expert_picks.shape
        shard_picks = capacity // group_size
        loss_scale = 1.0 / math.sqrt(tok_dev * group_size * hidden)
        my_index = lax.axis_index('ep')
        expert_col = jnp.arange(group_size)[None, :, None] * local_experts + jnp.arange(local_experts)[:, None, None]

        wanted = expert_picks.reshape(local_experts, group_size, shard_picks)
        asked_ids = lax.all_to_all(wanted, 'ep', 1, 1, tiled=True) - my_index * tok_dev
        flat_ids = asked_ids.reshape(-1)

        logits = jnp.dot(x, gate_w, preferred_element_type=jnp.float32)
        gate_probs = jax.nn.softmax(logits, axis=-1)
        gate_vals = gate_probs[asked_ids, expert_col]
        tok_rows = lax.all_to_all(x[asked_ids], 'ep', 1, 1, tiled=True).reshape(local_experts, capacity, hidden)

        pre_act = jnp.einsum('lch,lhf->lcf', tok_rows, up_w, preferred_element_type=jnp.float32)
        gelu_val, gelu_pull = jax.vjp(jax.nn.gelu, pre_act)
        hidden_act = gelu_val.astype(jnp.bfloat16)
        expert_out = jnp.einsum('lcf,lfh->lch', hidden_act, down_w, preferred_element_type=jnp.float32).astype(jnp.bfloat16)
        out_back = lax.all_to_all(expert_out.reshape(local_experts, group_size, shard_picks, hidden), 'ep', 1, 1, tiled=True).astype(jnp.float32)

        mixed_f32 = x.astype(jnp.float32) + jax.ops.segment_sum((gate_vals[..., None] * out_back).reshape(-1, hidden), flat_ids, num_segments=tok_dev)
        y = mixed_f32.astype(jnp.bfloat16)
        weight_f32 = loss_w.astype(jnp.float32)
        loss_total = lax.psum(jnp.sum(y.astype(jnp.float32) * weight_f32), 'ep') * loss_scale

        dy_rows = loss_w[asked_ids].astype(jnp.float32) * loss_scale
        grad_out = (gate_vals[..., None] * dy_rows).astype(jnp.bfloat16)
        grad_gate_vals = jnp.sum(dy_rows * out_back, axis=-1)
        grad_out_in = lax.all_to_all(grad_out, 'ep', 1, 1, tiled=True).reshape(local_experts, capacity, hidden)

        grad_down = jnp.einsum('lcf,lch->lfh', hidden_act, grad_out_in, preferred_element_type=jnp.float32).astype(jnp.bfloat16)
        grad_act = jnp.einsum('lch,lfh->lcf', grad_out_in, down_w, preferred_element_type=jnp.float32).astype(jnp.bfloat16)
        grad_pre = gelu_pull(grad_act.astype(jnp.float32))[0].astype(jnp.bfloat16)
        grad_up = jnp.einsum('lch,lcf->lhf', tok_rows, grad_pre, preferred_element_type=jnp.float32).astype(jnp.bfloat16)
        grad_rows = jnp.einsum('lcf,lhf->lch', grad_pre, up_w, preferred_element_type=jnp.float32).astype(jnp.bfloat16)
        rows_back = lax.all_to_all(grad_rows.reshape(local_experts, group_size, shard_picks, hidden), 'ep', 1, 1, tiled=True)

        probs_grad = jnp.zeros(gate_probs.shape, jnp.float32).at[asked_ids, expert_col].add(grad_gate_vals)
        grad_logits = (gate_probs * (probs_grad - jnp.sum(gate_probs * probs_grad, axis=-1, keepdims=True))).astype(jnp.bfloat16)
        grad_gate = lax.psum(lax.dot_general(x, grad_logits, (((0,), (0,)), ((), ())), preferred_element_type=jnp.float32), 'ep')
        grad_x = (weight_f32 * loss_scale
                  + jax.ops.segment_sum(rows_back.astype(jnp.float32).reshape(-1, hidden), flat_ids, num_segments=tok_dev)
                  + lax.dot_general(grad_logits, gate_w, (((1,), (1,)), ((), ())), preferred_element_type=jnp.float32))
        return y, loss_total, grad_x.astype(jnp.bfloat16), grad_up, grad_down, grad_gate

    return jax.shard_map(device_step, mesh=mesh,
                         in_specs=(P('ep'), P(), P('ep'), P('ep'), P('ep'), P('ep')),
                         out_specs=(P('ep'), P(), P('ep'), P('ep'), P('ep'), P()),
                         check_vma=False)
```

profile of v0, /device:TPU:0, one launch (start us, length us, event | category | flops | bytes accessed | tf_op | source)
XLA Modules:
  0.0 621.1 jit_solution(2201720050062041280)
XLA Ops:
  8.6 7.4 %all-to-all-start = ((s32[2,32,32]{2,0,1:T(2,128)}), s32[2,32,32]{2,0,1:T(2,128)S(1)}, u32[]{:S(2)}, u32[]{:S(2)}) async-start(s32[2,32,32]{2,0,1:T(2,128)} %copy.61), calls=%async_computation | async-start | bytes 65536 | tf_op jit(solution)/shard_map/all_to_all | solution.py:20
  16.0 7.1 %all-to-all-done = s32[2,32,32]{2,0,1:T(2,128)S(1)} async-done(((s32[2,32,32]{2,0,1:T(2,128)}), s32[2,32,32]{2,0,1:T(2,128)S(1)}, u32[]{:S(2)}, u32[]{:S(2)}) %all-to-all-start) | async-done | bytes 8224 | tf_op jit(solution)/shard_map/all_to_all | solution.py:20
  23.9 10.1 %gather_fusion.1 = bf16[2048,768]{1,0:T(8,128)(2,1)S(1)} fusion(bf16[1024,768]{1,0:T(8,128)(2,1)} %param.6, s32[2048]{0:T(1024)S(1)} %broadcast_clamp_fusion), kind=kCustom, calls=%fused_computation.1 | custom fusion | bytes 6299648 | tf_op jit(solution)/shard_map/gather | solution.py:26
  34.2 74.4 %all_to_all.25 = bf16[2,32,32,768]{3,2,0,1:T(8,128)(2,1)S(1)} all-to-all(bf16[2,32,32,768]{3,2,0,1:T(8,128)(2,1)S(1)} %copy.66), channel_id=1, replica_groups=mesh['ep'=32] {'ep'}, dimensions={1} | all-to-all | bytes 6291456 | tf_op jit(solution)/shard_map/all_to_all | solution.py:26
  110.5 13.3 %fusion.23 = f32[2,1024,3072]{2,1,0:T(8,128)} fusion(bf16[2,1024,768]{2,1,0:T(8,128)(2,1)S(1)} %bitcast.48, bf16[2,768,3072]{2,1,0:T(8,128)(2,1)S(1)} %copy-done.14), kind=kOutput, calls=%fused_computation.59 | convolution fusion | flops 9663676416 | bytes 37748736 | tf_op jit(solution)/shard_map/lch,lhf->lcf/dot_general | solution.py:28
  123.8 18.8 %convolution_convert_fusion.3 = bf16[2,1024,768]{2,1,0:T(8,128)(2,1)S(1)} fusion(bf16[2,3072,768]{2,1,0:T(8,128)(2,1)} %param.9, f32[2,1024,3072]{2,1,0:T(8,128)} %fusion.23), kind=kOutput, calls=%fused_computation.32 | convolution fusion | flops 9721872384 | bytes 37748736 | tf_op jit(solution)/shard_map/lcf,lfh->lch/dot_general | solution.py:31
  144.6 3.9 all-to-all-start.2
  151.3 9.4 %gather_fusion.2 = bf16[2048,768]{1,0:T(8,128)(2,1)} fusion(bf16[1024,768]{1,0:T(8,128)(2,1)S(1)} %copy-done.5, s32[2048]{0:T(1024)S(1)} %broadcast_clamp_fusion), kind=kCustom, calls=%fused_computation.2 | custom fusion | bytes 6299648 | tf_op jit(solution)/shard_map/gather | solution.py:39
  160.9 5.4 bitcast_convert_fusion
  166.3 54.0 %all-to-all-done.2 = bf16[2,32,32,768]{3,2,0,1:T(8,128)(2,1)} async-done(((bf16[2,32,32,768]{3,2,0,1:T(8,128)(2,1)}), bf16[2,32,32,768]{3,2,0,1:T(8,128)(2,1)}, u32[]{:S(2)}, u32[]{:S(2)}) %all-to-all-start.2) | async-done | bytes 3145760 | tf_op jit(solution)/shard_map/all_to_all | solution.py:32
  220.3 4.6 fusion.10
  225.0 14.5 %scatter_custom_fusion.2 = f32[65536]{0:T(1024)S(1)} fusion(s32[2048]{0:T(1024)S(1)} %reshape.129, f32[2048]{0:T(1024)S(1)} %reshape.131, f32[]{:T(128)} %constant.17.clone.1), kind=kCustom, calls=%fused_computation.42 | custom fusion | flops 2048 | bytes 262148
  240.3 16.8 %gather_fusion = f32[2048]{0:T(1024)S(1)} fusion(f32[1024,64]{0,1:T(8,128)S(1)} %get-tuple-element.7, s32[2048]{0:T(1024)S(1)} %reshape.91), kind=kCustom, calls=%fused_computation | custom fusion | bytes 32768 | tf_op jit(solution)/shard_map/gather | solution.py:25
  274.2 15.6 %scatter_fusion = f32[1024,768]{1,0:T(8,128)S(1)} fusion(f32[1024,768]{1,0:T(8,128)S(1)} %convert_element_type.52, s32[2048]{0:T(1024)S(1)} %reshape.115, f32[2048,768]{1,0:T(8,128)} %bitcast.46), kind=kCustom, calls=%fused_computation.3 | custom fusion | flops 1572864 | bytes 18882560 | tf_op jit(solution)/shard_map/scatter-add | solution.py:34
  298.0 38.4 %all-to-all-done.3 = bf16[2,32,32,768]{3,2,0,1:T(8,128)(2,1)} async-done(((bf16[2,32,32,768]{3,2,0,1:T(8,128)(2,1)}), bf16[2,32,32,768]{3,2,0,1:T(8,128)(2,1)}, u32[]{:S(2)}, u32[]{:S(2)}) %all-to-all-start.3) | async-done | bytes 3145760 | tf_op jit(solution)/shard_map/all_to_all | solution.py:42
  336.4 3.8 copy.75
  340.2 30.3 %fusion.2 = bf16[2,1024,3072]{2,1,0:T(8,128)(2,1)} fusion(f32[2,1024,3072]{2,1,0:T(8,128)} %fusion.23, bf16[2,1024,768]{2,1,0:T(8,128)(2,1)} %bitcast.50, bf16[2,3072,768]{2,1,0:T(8,128)(2,1)} %param.9), kind=kOutput, calls=%fused_computation.12 | convolution fusion | flops 9802088448 | bytes 50331648 | tf_op jit(solution)/shard_map/lch,lfh->lcf/dot_general | solution.py:45
  370.5 15.7 %convolution_convert_fusion.2 = bf16[2,1024,768]{2,1,0:T(8,128)(2,1)S(1)} fusion(bf16[2,1024,3072]{2,1,0:T(8,128)(2,1)} %fusion.2, bf16[2,768,3072]{2,1,0:T(8,128)(2,1)} %param.8), kind=kOutput, calls=%fused_computation.31 | convolution fusion | flops 9665249280 | bytes 25165824 | tf_op jit(solution)/shard_map/lcf,lhf->lch/dot_general | solution.py:48
  394.4 89.1 %psum.14 = f32[]{:T(128)} all-reduce(f32[]{:T(128)} %get-tuple-element.10), channel_id=1, replica_groups=mesh['ep'=32] {'ep'}, use_global_device_ids=true, to_apply=%region_4.0 | all-reduce | flops 1 | bytes 8 | tf_op jit(solution)/shard_map/psum | solution.py:37
  484.1 23.9 %convolution_convert_fusion = bf16[2,3072,768]{2,1,0:T(8,128)(2,1)} fusion(bf16[2,1024,768]{2,1,0:T(8,128)(2,1)} %bitcast.51, f32[2,1024,3072]{2,1,0:T(8,128)} %fusion.23), kind=kOutput, calls=%fused_computation.23 | convolution fusion | flops 9725018112 | bytes 37748736 | tf_op jit(solution)/shard_map/lcf,lch->lfh/dot_general | solution.py:44
  508.0 17.8 %convolution_convert_fusion.1 = bf16[2,768,3072]{2,1,0:T(8,128)(2,1)} fusion(bf16[2,1024,768]{2,1,0:T(8,128)(2,1)} %bitcast.49, bf16[2,1024,3072]{2,1,0:T(8,128)(2,1)} %fusion.2), kind=kOutput, calls=%fused_computation.24 | convolution fusion | flops 9668395008 | bytes 25165824 | tf_op jit(solution)/shard_map/lch,lcf->lhf/dot_general | solution.py:47
  525.8 5.4 copy.77
  531.2 15.6 %scatter_fusion.1 = f32[1024,768]{1,0:T(8,128)S(1)} fusion(f32[1024,768]{1,0:T(8,128)S(1)} %fusion.12, s32[2048]{0:T(1024)S(1)} %reshape.115, f32[2048,768]{1,0:T(8,128)} %bitcast.45), kind=kCustom, calls=%fused_computation.4 | custom fusion | flops 1572864 | bytes 18882560 | tf_op jit(solution)/shard_map/scatter-add | solution.py:55
  548.1 63.2 %all-reduce.2.cloned.1.call-done = f32[768,64]{0,1:T(8,128)} async-done(((f32[768,64]{0,1:T(8,128)}), f32[768,64]{0,1:T(8,128)}) %all-reduce.2.cloned.1.call-update) | async-done | bytes 196624 | tf_op jit(solution)/shard_map/psum | solution.py:53
  (79 shorter events, 46.3 us)
Async XLA Ops:
  7.2 141.3 %copy-start = (bf16[768,64]{0,1:T(8,128)(2,1)S(1)}, bf16[768,64]{0,1:T(8,128)(2,1)}, u32[]{:S(2)}) copy-start(bf16[768,64]{0,1:T(8,128)(2,1)} %param.7) | copy-start | bytes 294916
  8.6 14.5 %all-to-all-start = ((s32[2,32,32]{2,0,1:T(2,128)}), s32[2,32,32]{2,0,1:T(2,128)S(1)}, u32[]{:S(2)}, u32[]{:S(2)}) async-start(s32[2,32,32]{2,0,1:T(2,128)} %copy.61), calls=%async_computation | async-start | bytes 65536 | tf_op jit(solution)/shard_map/all_to_all | solution.py:20
  34.2 76.3 %copy-start.14 = (bf16[2,768,3072]{2,1,0:T(8,128)(2,1)S(1)}, bf16[2,768,3072]{2,1,0:T(8,128)(2,1)}, u32[]{:S(2)}) copy-start(bf16[2,768,3072]{2,1,0:T(8,128)(2,1)} %param.8) | copy-start | bytes 28311556
  108.9 1.6 copy-start.8
  142.7 5.8 copy-start.4
  142.7 7.6 %copy-start.13 = (s32[2]{0:T(128)S(1)}, s32[2]{0:T(128)}, u32[]{:S(2)}) copy-start(s32[2]{0:T(128)} %constant.43) | copy-start | bytes 28
  142.7 8.6 %copy-start.5 = (bf16[1024,768]{1,0:T(8,128)(2,1)S(1)}, bf16[1024,768]{1,0:T(8,128)(2,1)}, u32[]{:S(2)}) copy-start(bf16[1024,768]{1,0:T(8,128)(2,1)} %param.11) | copy-start | bytes 4718596
  144.6 75.7 %all-to-all-start.2 = ((bf16[2,32,32,768]{3,2,0,1:T(8,128)(2,1)}), bf16[2,32,32,768]{3,2,0,1:T(8,128)(2,1)}, u32[]{:S(2)}, u32[]{:S(2)}) async-start(bf16[2,32,32,768]{3,2,0,1:T(8,128)(2,1)} %copy.68), calls=%async_computation.2 | async-start | bytes 6291456 | tf_op jit(solution)/shard_map/all_to_all | solution.py:32
  239.6 0.7 copy-start.9
  240.3 18.3 %copy-start.7 = (bf16[2048,768]{1,0:T(8,128)(2,1)S(1)}, bf16[2048,768]{1,0:T(8,128)(2,1)}, u32[]{:S(2)}) copy-start(bf16[2048,768]{1,0:T(8,128)(2,1)} %gather_fusion.2) | copy-start | bytes 9437188
  260.8 75.6 %all-to-all-start.3 = ((bf16[2,32,32,768]{3,2,0,1:T(8,128)(2,1)}), bf16[2,32,32,768]{3,2,0,1:T(8,128)(2,1)}, u32[]{:S(2)}, u32[]{:S(2)}) async-start(bf16[2,32,32,768]{3,2,0,1:T(8,128)(2,1)} %multiply_convert_fusion.1), calls=%async_computation.3 | async-start | bytes 6291456 | tf_op jit(solution)/shard_map/all_to_all | solution.py:42
  274.2 17.3 %copy-start.12 = (f32[1024]{0:T(1024)S(1)}, f32[1024]{0:T(1024)}, u32[]{:S(2)}) copy-start(f32[1024]{0:T(1024)} %get-tuple-element.6) | copy-start | bytes 12292
  289.8 1.7 copy-start.2
  289.8 5.5 copy-start.6
  292.5 0.7 copy-start.10
  293.1 2.4 copy-start.3
  386.2 5.7 copy-start.11
  388.1 137.6 %all-to-all-start.4 = ((bf16[2,32,32,768]{3,2,0,1:T(8,128)(2,1)}), bf16[2,32,32,768]{3,2,0,1:T(8,128)(2,1)}, u32[]{:S(2)}, u32[]{:S(2)}) async-start(bf16[2,32,32,768]{3,2,0,1:T(8,128)(2,1)} %copy.76), calls=%async_computation.4 | async-start | bytes 6291456 | tf_op jit(solution)/shard_map/all_to_all | solution.py:49
  391.7 219.6 %all-reduce.2.cloned.1.call-start = ((), (), s32[]{:S(2)}) async-start(), calls=%async_computation.5 | async-start | bytes 393216 | tf_op jit(solution)/shard_map/psum | solution.py:53
  531.2 81.7 %copy-start.1 = (bf16[768,64]{0,1:T(8,128)(2,1)S(1)}, bf16[768,64]{0,1:T(8,128)(2,1)}, u32[]{:S(2)}) copy-start(bf16[768,64]{0,1:T(8,128)(2,1)} %param.7) | copy-start | bytes 294916
Sparse Core Ops, SparseCore 0:
  483.7 127.5 all-reduce.1
where the time goes:
time: 629 us; the launch traced here: 621 us
  waiting for transfers between devices  163 us (26%)
  blocking collectives  163 us (26%)
  matrix products  125 us (20%)
  other arithmetic  71.2 us (11%)
  local copies, waits for them, and re-layouts  63.8 us (10%)
  starting transfers between devices  18.8 us (3%)
  between operations  16.6 us (3%)
    psum x1, blocking collectives, device_step(): lax.psum(jnp.sum(y.astype(jnp.float32) * weight_f32), 'ep') * loss_scale  89 us
    all_to_all x1, blocking collectives, device_step(): lax.all_to_all(x[asked_ids], 'ep', 1, 1, tiled=True)  74.4 us
    psum x1, waiting for transfers between devices, device_step(): lax.psum(lax.dot_general(x, grad_logits, (((0,), (0,)), ((), ())), prefer...  63.1 us
    all_to_all x1, waiting for transfers between devices, device_step(): lax.all_to_all(expert_out.reshape(local_experts, group_size, shard_picks,...  54.1 us
    all_to_all x1, waiting for transfers between devices, device_step(): lax.all_to_all(grad_out, 'ep', 1, 1, tiled=True)  38.4 us
    dot_general x1, matrix products, device_step(): jnp.einsum('lch,lfh->lcf', grad_out_in, down_w, preferred_element_type=jn...  30.1 us
    dot_general x1, matrix products, device_step(): jnp.einsum('lcf,lch->lfh', hidden_act, grad_out_in, preferred_element_typ...  23.9 us
    dot_general x1, matrix products, device_step(): jnp.einsum('lcf,lfh->lch', hidden_act, down_w, preferred_element_type=jnp...  18.8 us
  transfers between devices with their start and end apart: 5, of which 4 were waited for; matrix products, arithmetic and copies ran while one was open for 19% of the time, Pallas kernels for 0%

commit v1 on v0

v1 whole, which is shorter than its diff:
```python
import math
import jax
import jax.numpy as jnp
from jax import lax
from jax.sharding import PartitionSpec as P

F32 = jnp.float32
BF16 = jnp.bfloat16


def split3(v):
    hi = lax.reduce_precision(v, 8, 7)
    rest = v - hi
    mid = lax.reduce_precision(rest, 8, 7)
    return hi.astype(BF16), mid.astype(BF16), (rest - mid).astype(BF16)


def dot(a, b, ca, cb):
    return lax.dot_general(a, b, (((ca,), (cb,)), ((), ())), preferred_element_type=F32)


def solution(mesh):
    group_size = mesh.shape['ep']

    def device_step(x, gate_w, up_w, down_w, expert_picks, loss_w):
        tok_dev, hidden = x.shape
        local_experts, capacity = expert_picks.shape
        shard_picks = capacity // group_size
        experts = gate_w.shape[1]
        loss_scale = 1.0 / math.sqrt(tok_dev * group_size * hidden)
        my_index = lax.axis_index('ep')

        def exchange(rows):
            return lax.all_to_all(rows.reshape(group_size, shard_picks, -1), 'ep', 0, 0, tiled=True).reshape(capacity, -1)

        def softmax_rows(rows):
            return jax.nn.softmax(dot(rows, gate_w, 1, 0), axis=-1)

        ids = lax.all_to_all(expert_picks[0].reshape(group_size, shard_picks), 'ep', 0, 0, tiled=True)
        slot_tok = ids.reshape(-1) - my_index * tok_dev
        pick = (slot_tok[:, None] == jnp.arange(tok_dev)[None, :]).astype(BF16)
        x_out = dot(pick, x, 1, 0).astype(BF16)
        r_out = dot(pick, loss_w, 1, 0).astype(BF16)
        x_in = exchange(x_out)
        r_in = exchange(r_out)

        probs_in = softmax_rows(x_in)
        dy_in = r_in.astype(F32) * loss_scale
        cols = jnp.arange(experts)[None, :]
        kept = []
        for l in range(local_experts):
            gate = jnp.sum(jnp.where(cols == my_index * local_experts + l, probs_in, 0.0), axis=1)
            pre = dot(x_in, up_w[l], 1, 0)
            act, pull = jax.vjp(jax.nn.gelu, pre)
            act = act.astype(BF16)
            h = dot(act, down_w[l], 1, 0).astype(BF16)
            kept.append((gate, act, pull, exchange(h)))

        g_back, grad_up, grad_down = [], [], []
        for l in range(local_experts):
            gate, act, pull, _ = kept[l]
            dh = (gate[:, None] * dy_in).astype(BF16)
            du = dot(dh, down_w[l], 1, 1).astype(BF16)
            da = pull(du.astype(F32))[0].astype(BF16)
            g = dot(da, up_w[l], 1, 1).astype(BF16)
            g_back.append(exchange(g))
            grad_down.append(dot(act, dh, 0, 0).astype(BF16))
            grad_up.append(dot(x_in, da, 0, 0).astype(BF16))

        probs = softmax_rows(x)
        slot_dev = jnp.arange(capacity) // shard_picks
        parts = jnp.concatenate(split3(probs), axis=1)
        slot_probs = dot(pick, parts, 1, 0).reshape(capacity, 3, experts)
        slot_probs = slot_probs[:, 0] + slot_probs[:, 1] + slot_probs[:, 2]
        mixed = 0.0
        d_slot = 0.0
        for l in range(local_experts):
            h_l = kept[l][3].astype(F32)
            here = cols == (slot_dev * local_experts + l)[:, None]
            gate_l = jnp.sum(jnp.where(here, slot_probs, 0.0), axis=1)
            mixed += gate_l[:, None] * h_l
            d_gate = jnp.sum(r_out.astype(F32) * loss_scale * h_l, axis=1)
            d_slot += jnp.where(here, d_gate[:, None], 0.0)
        m1, m2, m3 = split3(mixed)
        y = (x.astype(F32) + (dot(pick, m1, 0, 0) + dot(pick, m2, 0, 0) + dot(pick, m3, 0, 0))).astype(BF16)
        weight = loss_w.astype(F32)
        loss_part = jnp.sum(y.astype(F32) * weight) * loss_scale

        d_parts = dot(pick, jnp.concatenate(split3(d_slot), axis=1), 0, 0).reshape(tok_dev, 3, experts)
        d_probs = d_parts[:, 0] + d_parts[:, 1] + d_parts[:, 2]
        d_logits = (probs * (d_probs - jnp.sum(probs * d_probs, axis=-1, keepdims=True))).astype(BF16)
        gate_part = dot(x, d_logits, 0, 0).reshape(group_size, -1, experts)
        small = jnp.concatenate([gate_part, jnp.broadcast_to(loss_part, (group_size, 1, experts))], axis=1)
        small = jnp.sum(lax.all_to_all(small, 'ep', 0, 0, tiled=True).reshape(group_size, -1, experts), axis=0)
        loss = small[-1, 0]
        grad_gate = lax.all_gather(small[:-1], 'ep', axis=0, tiled=True)

        grad_x = (weight * loss_scale + sum(dot(pick, g, 0, 0) for g in g_back) + dot(d_logits, gate_w, 1, 1)).astype(BF16)
        return y, loss, grad_x, jnp.stack(grad_up), jnp.stack(grad_down), grad_gate

    return jax.shard_map(device_step, mesh=mesh,
                         in_specs=(P('ep'), P(), P('ep'), P('ep'), P('ep'), P('ep')),
                         out_specs=(P('ep'), P(), P('ep'), P('ep'), P('ep'), P()),
                         check_vma=False)
```

time: 629 us -> 422 us (0.67)
  waiting for transfers between devices: 163 us -> 67 us
  blocking collectives: 163 us -> 108 us
  local copies, waits for them, and re-layouts: 63.8 us -> 13.2 us
  other arithmetic: 71.2 us -> 23.7 us
  matrix products: 125 us -> 172 us
  between operations: 16.6 us -> 2.08 us
  starting transfers between devices: 18.8 us -> 29.3 us
    psum x1 -> x0, blocking collectives: 89 us -> none  [device_step(): lax.psum(jnp.sum(y.astype(jnp.float32) * weight_f32), 'ep') * loss_scale]
    psum x1 -> x0, waiting for transfers between devices: 63.1 us -> none  [device_step(): lax.psum(lax.dot_general(x, grad_logits, (((0,), (0,)), ((), ())), prefer...]
    all_gather x0 -> x1, blocking collectives: none -> 55.1 us  [device_step(): grad_gate = lax.all_gather(small[:-1], 'ep', axis=0, tiled=True)]
    dot_general x9 -> x25, matrix products: 125 us -> 172 us  [dot(): lax.dot_general(a, b, (((ca,), (cb,)), ((), ())), preferred_element_type=...]
    gather x6 -> x0, local copies, waits for them, and re-layouts: 38 us -> none  [the longest x3 18.3 us: device_step(): gate_vals = gate_probs[asked_ids, expert_col]]
    all_to_all x4 -> x6, waiting for transfers between devices: 99.6 us -> 67 us  [the longest x5 60 us: exchange(): lax.all_to_all(rows.reshape(group_size, shard_picks, -1), 'ep', 0, 0, til...]
    scatter-add x2 -> x0, other arithmetic: 31.3 us -> none  [the longest x1 15.6 us: device_step(): jax.ops.segment_sum((gate_vals[..., None] * out_back).reshape(-1, hidden)...]
    all_to_all x1 -> x2, blocking collectives: 74.4 us -> 52.9 us  [the longest x1 39.8 us: exchange(): lax.all_to_all(rows.reshape(group_size, shard_picks, -1), 'ep', 0, 0, til...]
  transfers between devices with their start and end apart: 5 -> 6, of which waited for: 4 -> 4; matrix products, arithmetic and copies ran while one was open for 19% -> 23% of each run, Pallas kernels for 0% -> 0%
where the time goes in v1:
time: 422 us; the launch traced here: 415 us
  matrix products  172 us (41%)
  blocking collectives  108 us (26%)
  waiting for transfers between devices  67 us (16%)
  starting transfers between devices  29.3 us (7%)
  other arithmetic  23.7 us (6%)
  local copies, waits for them, and re-layouts  13.2 us (3%)
    dot_general x25, matrix products, dot(): lax.dot_general(a, b, (((ca,), (cb,)), ((), ())), preferred_element_type=...  172 us
    all_to_all x5, waiting for transfers between devices, exchange(): lax.all_to_all(rows.reshape(group_size, shard_picks, -1), 'ep', 0, 0, til...  60 us
    all_gather x1, blocking collectives, device_step(): grad_gate = lax.all_gather(small[:-1], 'ep', axis=0, tiled=True)  55.1 us
    all_to_all x1, blocking collectives, exchange(): lax.all_to_all(rows.reshape(group_size, shard_picks, -1), 'ep', 0, 0, til...  39.8 us
    all_to_all x5, starting transfers between devices, exchange(): lax.all_to_all(rows.reshape(group_size, shard_picks, -1), 'ep', 0, 0, til...  21.9 us
    all_to_all x1, blocking collectives, device_step(): lax.all_to_all(small, 'ep', 0, 0, tiled=True)  13.1 us
    unnamed x37, local copies, waits for them, and re-layouts  8.53 us
  transfers between devices with their start and end apart: 6, of which 4 were waited for; matrix products, arithmetic and copies ran while one was open for 23% of the time, Pallas kernels for 0%

profile of v1, /device:TPU:0, one launch (start us, length us, event | category | flops | bytes accessed | tf_op | source)
XLA Modules:
  0.0 415.5 jit_solution(15164557003313820856)
XLA Ops:
  2.1 7.4 %all-to-all-start = ((s32[32,1,32]{2,1,0:T(1,128)}), s32[32,1,32]{2,1,0:T(1,128)S(1)}, u32[]{:S(2)}, u32[]{:S(2)}) async-start(s32[32,1,32]{2,1,0:T(1,128)} %all_to_all.27), calls=%async_computation | async-start | bytes 32768 | tf_op jit(solution)/shard_map/all_to_all | solution.py:39
  9.5 7.1 %all-to-all-done = s32[32,1,32]{2,1,0:T(1,128)S(1)} async-done(((s32[32,1,32]{2,1,0:T(1,128)}), s32[32,1,32]{2,1,0:T(1,128)S(1)}, u32[]{:S(2)}, u32[]{:S(2)}) %all-to-all-start) | async-done | bytes 4128 | tf_op jit(solution)/shard_map/all_to_all | solution.py:39
  20.2 39.8 %all_to_all.44 = bf16[32,32,768]{2,1,0:T(8,128)(2,1)S(1)} all-to-all(bf16[32,32,768]{2,1,0:T(8,128)(2,1)S(1)} %bitcast.114), channel_id=1, replica_groups=mesh['ep'=32] {'ep'}, dimensions={0} | all-to-all | bytes 3145728 | tf_op jit(solution)/shard_map/all_to_all | solution.py:34
  60.0 7.9 %fusion.25 = f32[1024,3072]{1,0:T(8,128)} fusion(bf16[1024,768]{1,0:T(8,128)(2,1)S(1)} %bitcast.102, bf16[2,768,3072]{2,1,0:T(8,128)(2,1)S(1)} %copy-done.7), kind=kOutput, calls=%fused_computation.41 | convolution fusion | flops 4831838208 | bytes 18874368 | tf_op jit(solution)/shard_map/dot_general | solution.py:19
  68.0 11.2 %fusion.87 = bf16[1024,768]{1,0:T(8,128)(2,1)} fusion(bf16[2,3072,768]{2,1,0:T(8,128)(2,1)S(1)} %bitcast.120, f32[1024,3072]{1,0:T(8,128)} %fusion.25), kind=kOutput, calls=%fused_computation.114 | convolution fusion | flops 4860936192 | bytes 18874368 | tf_op jit(solution)/shard_map/dot_general | solution.py:19
  84.1 6.9 %fusion.32 = f32[1024,3072]{1,0:T(8,128)S(1)} fusion(bf16[1024,768]{1,0:T(8,128)(2,1)S(1)} %bitcast.103, bf16[2,768,3072]{2,1,0:T(8,128)(2,1)} %param.8), kind=kOutput, calls=%fused_computation.48 | convolution fusion | flops 4831838208 | bytes 18874368 | tf_op jit(solution)/shard_map/dot_general | solution.py:19
  95.4 10.9 %fusion.81 = bf16[1024,768]{1,0:T(8,128)(2,1)} fusion(bf16[2,3072,768]{2,1,0:T(8,128)(2,1)} %param.9, f32[1024,3072]{1,0:T(8,128)S(1)} %fusion.32), kind=kOutput, calls=%fused_computation.112 | convolution fusion | flops 4860936192 | bytes 18874368 | tf_op jit(solution)/shard_map/dot_general | solution.py:19
  106.4 15.3 %all-to-all-done.3 = bf16[32,32,768]{2,1,0:T(8,128)(2,1)} async-done(((bf16[32,32,768]{2,1,0:T(8,128)(2,1)}), bf16[32,32,768]{2,1,0:T(8,128)(2,1)}, u32[]{:S(2)}, u32[]{:S(2)}) %all-to-all-start.3) | async-done | bytes 1572896 | tf_op jit(solution)/shard_map/all_to_all | solution.py:34
  125.8 37.3 %all-to-all-done.2 = bf16[32,32,768]{2,1,0:T(8,128)(2,1)} async-done(((bf16[32,32,768]{2,1,0:T(8,128)(2,1)}), bf16[32,32,768]{2,1,0:T(8,128)(2,1)}, u32[]{:S(2)}, u32[]{:S(2)}) %all-to-all-start.2) | async-done | bytes 1572896 | tf_op jit(solution)/shard_map/all_to_all | solution.py:34
  171.6 6.4 %fusion.42 = f32[1024,768]{1,0:T(8,128)} fusion(s32[1024]{0:T(1024)S(1)} %sub.75, bf16[1024,768]{1,0:T(8,128)(2,1)} %bitcast.13, bf16[1024,768]{1,0:T(8,128)(2,1)} %bitcast.12, f32[1024]{0:T(1024)S(1)} %get-tuple-element.15, f32[1024]{0:T(1024)S(1)} %get-tuple-element.14), kind=kOutput, calls=%fused_computation.63 | convolution fusion | flops 1619525632 | bytes 6303744 | tf_op jit(solution)/shard_map/dot_general | solution.py:19
  185.6 9.1 %fusion.55 = (f32[]{:T(128)}, bf16[1024,768]{1,0:T(8,128)(2,1)}) fusion(bf16[1024,768]{1,0:T(8,128)(2,1)} %param.11, f32[1024,768]{1,0:T(8,128)} %fusion.42, f32[1024,768]{1,0:T(8,128)} %fusion.43, bf16[1024,768]{1,0:T(8,128)(2,1)} %bitcast.13, bf16[1024,768]{1,0:T(8,128)(2,1)} %bitcast.12, f32[1024]{0:T(1024)S(1)} %get-tuple-element.15, ...), kind=kOutput, calls=%fused_computation.82 | convolution fusion | flops 1624244224 | bytes 14168068 | tf_op jit(solution)/shard_map/dot_general | solution.py:19
  196.7 13.1 %all_to_all.45 = f32[32,1,1600]{2,1,0:T(1,128)S(1)} all-to-all(f32[32,1,1600]{2,1,0:T(1,128)S(1)} %reshape.154), channel_id=1, replica_groups=mesh['ep'=32] {'ep'}, dimensions={0} | all-to-all | bytes 409600 | tf_op jit(solution)/shard_map/all_to_all | solution.py:94
  219.5 55.1 %all_gather.3 = f32[768,64]{1,0:T(8,128)} all-gather(f32[24,64]{1,0:T(8,128)S(1)} %slice.63), channel_id=1, replica_groups=mesh['ep'=32] {'ep'}, dimensions={0}, use_global_device_ids=true | all-gather | bytes 202752 | tf_op jit(solution)/shard_map/all_gather | solution.py:96
  278.0 15.9 %fusion.2 = bf16[1024,3072]{1,0:T(8,128)(2,1)} fusion(f32[1024,3072]{1,0:T(8,128)} %copy-done.10, bf16[1024,768]{1,0:T(8,128)(2,1)S(1)} %bitcast.117, bf16[2,3072,768]{2,1,0:T(8,128)(2,1)} %param.9), kind=kOutput, calls=%fused_computation.10 | convolution fusion | flops 4901044224 | bytes 25165824 | tf_op jit(solution)/shard_map/dot_general | solution.py:19
  294.0 8.7 %fusion.78 = bf16[1024,768]{1,0:T(8,128)(2,1)} fusion(bf16[1024,3072]{1,0:T(8,128)(2,1)} %fusion.2, bf16[2,768,3072]{2,1,0:T(8,128)(2,1)S(1)} %bitcast.122), kind=kOutput, calls=%fused_computation.111 | convolution fusion | flops 4832624640 | bytes 12582912 | tf_op jit(solution)/shard_map/dot_general | solution.py:19
  302.7 6.8 %fusion.34 = bf16[1,768,3072]{2,1,0:T(8,128)(2,1)} fusion(bf16[1024,768]{1,0:T(8,128)(2,1)S(1)} %bitcast.105, bf16[1024,3072]{1,0:T(8,128)(2,1)S(1)} %copy-done.9), kind=kOutput, calls=%fused_computation.54 | convolution fusion | flops 4834197504 | bytes 12582912 | tf_op jit(solution)/shard_map/dot_general | solution.py:19
  311.1 11.6 %fusion.36 = bf16[1,3072,768]{2,1,0:T(8,128)(2,1)} fusion(bf16[1024,768]{1,0:T(8,128)(2,1)S(1)} %get-tuple-element.18, f32[1024,3072]{1,0:T(8,128)} %copy-done.10), kind=kOutput, calls=%fused_computation.56 | convolution fusion | flops 4862509056 | bytes 18874368 | tf_op jit(solution)/shard_map/dot_general | solution.py:19
  327.2 15.4 %fusion.7 = bf16[1024,3072]{1,0:T(8,128)(2,1)S(1)} fusion(f32[1024,3072]{1,0:T(8,128)} %fusion.25, bf16[1024,768]{1,0:T(8,128)(2,1)} %bitcast.116, bf16[2,3072,768]{2,1,0:T(8,128)(2,1)} %param.9), kind=kOutput, calls=%fused_computation.15 | convolution fusion | flops 4901044224 | bytes 25165824 | tf_op jit(solution)/shard_map/dot_general | solution.py:19
  342.6 10.8 %fusion.84 = bf16[1024,768]{1,0:T(8,128)(2,1)} fusion(bf16[1024,3072]{1,0:T(8,128)(2,1)S(1)} %fusion.7, bf16[2,768,3072]{2,1,0:T(8,128)(2,1)} %param.8), kind=kOutput, calls=%fused_computation.113 | convolution fusion | flops 4832624640 | bytes 12582912 | tf_op jit(solution)/shard_map/dot_general | solution.py:19
  353.5 11.6 %fusion.37 = bf16[1,3072,768]{2,1,0:T(8,128)(2,1)} fusion(bf16[1024,768]{1,0:T(8,128)(2,1)S(1)} %copy-done.4, f32[1024,3072]{1,0:T(8,128)} %fusion.25), kind=kOutput, calls=%fused_computation.57 | convolution fusion | flops 4862509056 | bytes 18874368 | tf_op jit(solution)/shard_map/dot_general | solution.py:19
  371.4 8.4 %pad_maximum_fusion.1 = bf16[2,3072,768]{2,1,0:T(8,128)(2,1)} fusion(bf16[1,3072,768]{2,1,0:T(8,128)(2,1)} %fusion.37, bf16[1,3072,768]{2,1,0:T(8,128)(2,1)} %fusion.36), kind=kLoop, calls=%fused_computation.31 | loop fusion | flops 4718592 | bytes 18874368 | tf_op jit(solution)/shard_map/stack | solution.py:99
  379.8 9.5 %fusion.35 = bf16[1,768,3072]{2,1,0:T(8,128)(2,1)} fusion(bf16[1024,768]{1,0:T(8,128)(2,1)S(1)} %bitcast.106, bf16[1024,3072]{1,0:T(8,128)(2,1)} %copy-done.8), kind=kOutput, calls=%fused_computation.55 | convolution fusion | flops 4834197504 | bytes 12582912 | tf_op jit(solution)/shard_map/dot_general | solution.py:19
  389.3 8.4 %pad_maximum_fusion = bf16[2,768,3072]{2,1,0:T(8,128)(2,1)} fusion(bf16[1,768,3072]{2,1,0:T(8,128)(2,1)} %fusion.35, bf16[1,768,3072]{2,1,0:T(8,128)(2,1)} %fusion.34), kind=kLoop, calls=%fused_computation.30 | loop fusion | flops 4718592 | bytes 18874368 | tf_op jit(solution)/shard_map/stack | solution.py:99
  401.7 7.3 %all-to-all-done.7 = bf16[32,32,768]{2,1,0:T(8,128)(2,1)} async-done(((bf16[32,32,768]{2,1,0:T(8,128)(2,1)}), bf16[32,32,768]{2,1,0:T(8,128)(2,1)}, u32[]{:S(2)}, u32[]{:S(2)}) %all-to-all-start.7) | async-done | bytes 1572896 | tf_op jit(solution)/shard_map/all_to_all | solution.py:34
  (83 shorter events, 71.4 us)
Async XLA Ops:
  0.6 124.5 %copy-start = (bf16[768,64]{0,1:T(8,128)(2,1)S(1)}, bf16[768,64]{0,1:T(8,128)(2,1)}, u32[]{:S(2)}) copy-start(bf16[768,64]{0,1:T(8,128)(2,1)} %param.7) | copy-start | bytes 294916
  2.1 14.5 %all-to-all-start = ((s32[32,1,32]{2,1,0:T(1,128)}), s32[32,1,32]{2,1,0:T(1,128)S(1)}, u32[]{:S(2)}, u32[]{:S(2)}) async-start(s32[32,1,32]{2,1,0:T(1,128)} %all_to_all.27), calls=%async_computation | async-start | bytes 32768 | tf_op jit(solution)/shard_map/all_to_all | solution.py:39
  16.7 43.4 %copy-start.7 = (bf16[2,768,3072]{2,1,0:T(8,128)(2,1)S(1)}, bf16[2,768,3072]{2,1,0:T(8,128)(2,1)}, u32[]{:S(2)}) copy-start(bf16[2,768,3072]{2,1,0:T(8,128)(2,1)} %param.8) | copy-start | bytes 28311556
  20.2 47.8 %slice-start = ((s8[9437184]{0:T(1024)(128)(4,1)}), s8[4194304]{0:T(1024)(128)(4,1)S(1)}, s32[]{:S(2)}) async-start(s8[9437184]{0:T(1024)(128)(4,1)} %bitcast.119), calls=%async_computation.8 | async-start | bytes 8388608
  60.0 7.9 %slice-start.1 = ((s8[9437184]{0:T(1024)(128)(4,1)}), s8[4194304]{0:T(1024)(128)(4,1)S(1)}, s32[]{:S(2)}) async-start(s8[9437184]{0:T(1024)(128)(4,1)} %bitcast.119), calls=%async_computation.9 | async-start | bytes 8388608
  60.0 7.9 %slice-start.2 = ((s8[9437184]{0:T(1024)(128)(4,1)}), s8[1048576]{0:T(1024)(128)(4,1)S(1)}, s32[]{:S(2)}) async-start(s8[9437184]{0:T(1024)(128)(4,1)} %bitcast.119), calls=%async_computation.10 | async-start | bytes 2097152
  79.2 42.5 %all-to-all-start.3 = ((bf16[32,32,768]{2,1,0:T(8,128)(2,1)}), bf16[32,32,768]{2,1,0:T(8,128)(2,1)}, u32[]{:S(2)}, u32[]{:S(2)}) async-start(bf16[32,32,768]{2,1,0:T(8,128)(2,1)} %bitcast.10), calls=%async_computation.3 | async-start | bytes 3145728 | tf_op jit(solution)/shard_map/all_to_all | solution.py:34
  91.0 4.5 %copy-start.10 = (f32[1024,3072]{1,0:T(8,128)}, f32[1024,3072]{1,0:T(8,128)S(1)}, u32[]{:S(2)}) copy-start(f32[1024,3072]{1,0:T(8,128)S(1)} %fusion.32) | copy-start | bytes 37748740
  95.4 29.7 %copy-start.1 = (bf16[1024,768]{1,0:T(8,128)(2,1)S(1)}, bf16[1024,768]{1,0:T(8,128)(2,1)}, u32[]{:S(2)}) copy-start(bf16[1024,768]{1,0:T(8,128)(2,1)} %param.6) | copy-start | bytes 4718596
  121.7 41.5 %all-to-all-start.2 = ((bf16[32,32,768]{2,1,0:T(8,128)(2,1)}), bf16[32,32,768]{2,1,0:T(8,128)(2,1)}, u32[]{:S(2)}, u32[]{:S(2)}) async-start(bf16[32,32,768]{2,1,0:T(8,128)(2,1)} %bitcast.113), calls=%async_computation.2 | async-start | bytes 3145728 | tf_op jit(solution)/shard_map/all_to_all | solution.py:34
  170.4 13.9 %copy-start.5 = (bf16[1024,64]{0,1:T(8,128)(2,1)}, bf16[1024,64]{0,1:T(8,128)(2,1)S(1)}, u32[]{:S(2)}) copy-start(bf16[1024,64]{0,1:T(8,128)(2,1)S(1)} %get-tuple-element.22) | copy-start | bytes 393220
  209.7 66.7 %all-to-all-start.5 = ((bf16[32,32,768]{2,1,0:T(8,128)(2,1)}), bf16[32,32,768]{2,1,0:T(8,128)(2,1)S(1)}, u32[]{:S(2)}, u32[]{:S(2)}) async-start(bf16[32,32,768]{2,1,0:T(8,128)(2,1)} %bitcast.109), calls=%async_computation.5 | async-start | bytes 3145728 | tf_op jit(solution)/shard_map/all_to_all | solution.py:34
  276.4 17.5 %slice-start.3 = ((s8[9437184]{0:T(1024)(128)(4,1)}), s8[4194304]{0:T(1024)(128)(4,1)S(1)}, s32[]{:S(2)}) async-start(s8[9437184]{0:T(1024)(128)(4,1)} %bitcast.121), calls=%async_computation.11 | async-start | bytes 8388608
  278.0 15.9 %slice-start.4 = ((s8[9437184]{0:T(1024)(128)(4,1)}), s8[4194304]{0:T(1024)(128)(4,1)S(1)}, s32[]{:S(2)}) async-start(s8[9437184]{0:T(1024)(128)(4,1)} %bitcast.121), calls=%async_computation.12 | async-start | bytes 8388608
  278.0 15.9 %slice-start.5 = ((s8[9437184]{0:T(1024)(128)(4,1)}), s8[1048576]{0:T(1024)(128)(4,1)S(1)}, s32[]{:S(2)}) async-start(s8[9437184]{0:T(1024)(128)(4,1)} %bitcast.121), calls=%async_computation.13 | async-start | bytes 2097152
  293.9 8.7 %copy-start.9 = (bf16[1024,3072]{1,0:T(8,128)(2,1)S(1)}, bf16[1024,3072]{1,0:T(8,128)(2,1)}, u32[]{:S(2)}) copy-start(bf16[1024,3072]{1,0:T(8,128)(2,1)} %fusion.2) | copy-start | bytes 18874372
  322.7 42.4 %all-to-all-start.6 = ((bf16[32,32,768]{2,1,0:T(8,128)(2,1)}), bf16[32,32,768]{2,1,0:T(8,128)(2,1)S(1)}, u32[]{:S(2)}, u32[]{:S(2)}) async-start(bf16[32,32,768]{2,1,0:T(8,128)(2,1)} %bitcast.112), calls=%async_computation.6 | async-start | bytes 3145728 | tf_op jit(solution)/shard_map/all_to_all | solution.py:34
  342.6 10.9 %copy-start.8 = (bf16[1024,3072]{1,0:T(8,128)(2,1)}, bf16[1024,3072]{1,0:T(8,128)(2,1)S(1)}, u32[]{:S(2)}) copy-start(bf16[1024,3072]{1,0:T(8,128)(2,1)S(1)} %fusion.7) | copy-start | bytes 18874372
  342.6 10.8 %copy-start.4 = (bf16[1024,768]{1,0:T(8,128)(2,1)S(1)}, bf16[1024,768]{1,0:T(8,128)(2,1)}, u32[]{:S(2)}) copy-start(bf16[1024,768]{1,0:T(8,128)(2,1)} %get-tuple-element.19) | copy-start | bytes 4718596
  365.1 43.9 %all-to-all-start.7 = ((bf16[32,32,768]{2,1,0:T(8,128)(2,1)}), bf16[32,32,768]{2,1,0:T(8,128)(2,1)}, u32[]{:S(2)}, u32[]{:S(2)}) async-start(bf16[32,32,768]{2,1,0:T(8,128)(2,1)} %bitcast.111), calls=%async_computation.7 | async-start | bytes 3145728 | tf_op jit(solution)/shard_map/all_to_all | solution.py:34
  409.0 4.0 copy-start.2
  409.0 4.0 copy-start.3
  409.0 4.0 copy-start.6

commit v2 on v0

v2 whole, which is shorter than its diff:
```python
import functools
import math
import jax
import jax.numpy as jnp
from jax import lax
from jax.experimental import pallas as pl
from jax.experimental.pallas import tpu as pltpu
from jax.sharding import PartitionSpec as P

F32 = jnp.float32
BF16 = jnp.bfloat16
GROUP = 8
TILE = 512
LANES = 128
C0 = math.sqrt(2.0 / math.pi)
C1 = 0.044715


def dot(a, b, ca=1, cb=0):
    return lax.dot_general(a, b, (((ca,), (cb,)), ((), ())), preferred_element_type=F32)


def split3(v):
    hi = v.astype(BF16)
    rest = v - hi.astype(F32)
    mid = rest.astype(BF16)
    return hi, mid, (rest - mid.astype(F32)).astype(BF16)


def softmax(logits):
    e = jnp.exp(logits - jnp.max(logits, axis=1, keepdims=True))
    return e / jnp.sum(e, axis=1, keepdims=True)


def xor(a, b, bits):
    return sum(((a // (1 << i) + b // (1 << i)) % 2) * (1 << i) for i in range(bits))


def moe_kernel(n, loss_scale, ids, x, r, wg, w1, w2,
               y_out, gx_out, gu_out, gd_out, gg_out, loss_out,
               xr_v, w1_v, w2_v, pick, xr_s, xr_in, hs, h_in, gs, g_in, dh_v, s_in, s_own, u_t, da_t, acc, big, out_st,
               ids_in, ids_t, d_acc, dlog, red_s, red_in, swap_s, swap_in, all_s, all_in,
               load_sem, ids_ss, ids_rs, xr_ss, xr_rs, h_ss, h_rs, g_ss, g_rs, red_ss, red_rs, swap_ss, swap_rs, all_ss, all_rs, out_sem):
    me = lax.axis_index('ep')
    bits = n.bit_length() - 1
    stages = n // GROUP
    half = n // 2
    tok, hidden = xr_v.shape[1:]
    per = tok // n
    rows = GROUP * per
    local_experts, _, ffn = w1_v.shape
    tiles = ffn // TILE
    experts = wg.shape[0]
    most = pl.ds(0, n - 1)

    def peer(p):
        return xor(me, n - 1 - p, bits)

    def group(i):
        return xor(me // GROUP, stages - 1 - i, bits - 3)

    def remote(src, dst, ss, rs, d):
        return pltpu.make_async_remote_copy(src, dst, ss, rs, device_id=(d,), device_id_type=pl.DeviceIdType.MESH)

    def span(q):
        return pl.ds(pl.multiple_of(q * rows, rows), rows)

    loads = [pltpu.make_async_copy(x, xr_v.at[0], load_sem.at[0]), pltpu.make_async_copy(r, xr_v.at[1], load_sem.at[1]),
             pltpu.make_async_copy(w1, w1_v, load_sem.at[2]), pltpu.make_async_copy(w2, w2_v, load_sem.at[3])]
    for c in loads:
        c.start()

    barrier = pltpu.get_barrier_semaphore()

    @pl.loop(0, n - 1)
    def _(p):
        pl.semaphore_signal(barrier, inc=1, device_id=(peer(p),), device_id_type=pl.DeviceIdType.MESH)
    pl.semaphore_wait(barrier, n - 1)

    packed = LANES // per

    @pl.loop(0, n - 1)
    def _(p):
        d = peer(p)
        remote(ids.at[d // packed], ids_in.at[me], ids_ss, ids_rs, d).start()
    ids_in[me] = ids[me // packed]
    all_ids = remote(ids_in.at[most], ids_in.at[most], ids_ss, ids_rs, me)
    all_ids.wait_send()
    all_ids.wait_recv()
    flat = ids_in[...].reshape(n, LANES).astype(F32)
    ids_t[...] = jnp.transpose(jnp.concatenate([flat] * (LANES // n), axis=0))
    cols = ids_t[pl.ds(pl.multiple_of((me % packed) * per, per), per), :]
    lane = lax.broadcasted_iota(jnp.int32, (per, LANES), 1)
    tok_iota = (lax.broadcasted_iota(jnp.int32, (per, tok), 1) + me * tok).astype(F32)

    loads[0].wait()
    loads[1].wait()

    @pl.loop(0, 2 * stages + 1)
    def _(s):
        @pl.when(s < stages)
        def _():
            base = group(s % stages) * GROUP
            for j in range(GROUP):
                col = jnp.sum(jnp.where(lane == base + j, cols, 0.0), axis=1, keepdims=True)
                at = pl.multiple_of((base + j) * per, per)
                pick[pl.ds(at, per), :] = jnp.where(tok_iota == col, 1.0, 0.0).astype(BF16)

        @pl.when(s < 2 * stages)
        def _():
            w, q = s // stages, group(s % stages)
            xr_s[w, pl.ds(q * GROUP, GROUP)] = dot(pick[span(q), :], xr_v[w]).astype(BF16).reshape(GROUP, per, hidden)

        @pl.when(s > 0)
        def _():
            w, i = (s - 1) // stages, (s - 1) % stages

            @pl.loop(0, GROUP)
            def _(j):
                p = i * GROUP + j

                @pl.when(p < n - 1)
                def _():
                    d = peer(p)
                    remote(xr_s.at[w, d], xr_in.at[w, me], xr_ss, xr_rs.at[w * stages + i], d).start()

                @pl.when(p == n - 1)
                def _():
                    xr_in[w, me] = xr_s[w, me]

    @pl.loop(0, stages)
    def _(c):
        s_own[span(c), :] = softmax(dot(xr_v[0, span(c), :], wg[...], 1, 1))
    loads[2].wait()
    loads[3].wait()

    def await_group(ref, sem, i):
        for cond, size in ((i < stages - 1, GROUP), (i == stages - 1, GROUP - 1)):
            @pl.when(cond)
            def _():
                part = ref(pl.ds(group(i) * GROUP, size))
                remote(part, part, xr_ss, sem, me).wait_recv()

    def send_h(i):
        @pl.loop(0, GROUP)
        def _(j):
            p = i * GROUP + j

            @pl.when(p < n - 1)
            def _():
                d = peer(p)
                remote(hs.at[d], h_in.at[me], h_ss, h_rs, d).start()

            @pl.when(p == n - 1)
            def _():
                h_in[me] = hs[me]

    lane_e = lax.broadcasted_iota(jnp.int32, (rows, experts), 1)
    row_dev = lax.broadcasted_iota(jnp.int32, (rows, experts), 0) // per

    @pl.loop(0, stages)
    def _(i):
        q = group(i)
        await_group(lambda b: xr_in.at[0, b], xr_rs.at[i], i)
        xg = xr_in[0, pl.ds(q * GROUP, GROUP)].reshape(rows, hidden)
        s_in[span(q), :] = softmax(dot(xg, wg[...], 1, 1))

        @pl.when(i > 0)
        def _():
            send_h(i - 1)

        @pl.loop(0, local_experts)
        def _(l):
            acc[...] = jnp.zeros_like(acc)

            @pl.loop(0, tiles)
            def _(t):
                at = pl.ds(pl.multiple_of(t * TILE, TILE), TILE)
                a = dot(xg, w1_v[l, :, at])
                u = (0.5 * a * (1.0 + jnp.tanh(C0 * (a + C1 * (a * a * a))))).astype(BF16)
                acc[...] += dot(u, w2_v[l, at, :])
            hs[pl.ds(q * GROUP, GROUP), pl.ds(pl.multiple_of(l * per, per), per), :] = acc[...].astype(BF16).reshape(GROUP, per, hidden)

    @pl.loop(0, stages)
    def _(i):
        await_group(lambda b: xr_in.at[1, b], xr_rs.at[stages + i], i)

        @pl.when(i == 0)
        def _():
            send_h(stages - 1)

    def wide_of(l):
        return pl.ds(pl.multiple_of(l * per, per), per)

    def send_g(l, i, lo, hi):
        @pl.loop(lo, hi)
        def _(j):
            p = i * GROUP + j

            @pl.when(p < n - 1)
            def _():
                d = peer(p)
                remote(gs.at[l, d], g_in.at[l, me], g_ss, g_rs.at[l * stages + i], d).start()

            @pl.when(p == n - 1)
            def _():
                g_in[l, me] = gs[l, me]

    def grads_out(step):
        l, t = step // tiles, step % tiles
        at = pl.ds(pl.multiple_of(t * TILE, TILE), TILE)
        pltpu.make_async_copy(w1_v.at[l, :, at], gu_out.at[l, :, at], out_sem.at[0]).start()
        pltpu.make_async_copy(w2_v.at[l, at, :], gd_out.at[l, at, :], out_sem.at[1]).start()

    @pl.loop(0, local_experts)
    def _(l):
        @pl.loop(0, stages)
        def _(q):
            gate = jnp.sum(jnp.where(lane_e == me * local_experts + l, s_in[span(q), :], 0.0), axis=1, keepdims=True)
            dy = xr_in[1, pl.ds(q * GROUP, GROUP)].reshape(rows, hidden).astype(F32) * loss_scale
            dh_v[span(q), :] = (gate * dy).astype(BF16)
            big[span(q), :] = jnp.zeros((rows, hidden), F32)

        @pl.loop(0, tiles)
        def _(t):
            step = l * tiles + t
            at = pl.ds(pl.multiple_of(t * TILE, TILE), TILE)

            @pl.loop(0, stages)
            def _(q):
                up = w1_v[l, :, at]
                a = dot(xr_in[0, pl.ds(q * GROUP, GROUP)].reshape(rows, hidden), up)
                th = jnp.tanh(C0 * (a + C1 * (a * a * a)))
                side = 0.5 * (1.0 + th)
                u_t[span(q), :] = (a * side).astype(BF16)
                slope = side + 0.5 * a * (1.0 - th * th) * (C0 + (3.0 * C0 * C1) * (a * a))
                du = dot(dh_v[span(q), :], w2_v[l, at, :], 1, 1).astype(BF16).astype(F32)
                da = (slope * du).astype(BF16)
                da_t[span(q), :] = da
                big[span(q), :] += dot(da, up, 1, 1)

            @pl.when(step > 0)
            def _():
                grads_out(step - 1)

            @pl.loop(0, TILE // rows)
            def _(m):
                part = dot(u_t[:, span(m)], dh_v[...], 0, 0).astype(BF16)
                w2_v[l, pl.ds(pl.multiple_of(t * TILE + m * rows, rows), rows), :] = part

            @pl.loop(0, hidden // rows)
            def _(m):
                xm = xr_in[0, :, :, span(m)].reshape(tok, rows)
                w1_v[l, span(m), at] = dot(xm, da_t[...], 0, 0).astype(BF16)

        @pl.loop(0, stages)
        def _(q):
            gs[l, pl.ds(q * GROUP, GROUP)] = big[span(q), :].astype(BF16).reshape(GROUP, per, hidden)

        @pl.when(l < local_experts - 1)
        def _():
            @pl.loop(0, stages)
            def _(i):
                send_g(l, i, 0, GROUP)
    grads_out(local_experts * tiles - 1)

    all_h = remote(hs.at[most], h_in.at[most], h_ss, h_rs, me)
    all_h.wait_recv()

    @pl.loop(0, stages)
    def _(q):
        big[span(q), :] = xr_v[0, span(q), :].astype(F32)
        d_acc[span(q), :] = jnp.zeros((rows, 3 * experts), F32)

    @pl.loop(0, stages)
    def _(q):
        blocks = pl.ds(q * GROUP, GROUP)
        slot_probs = softmax(dot(xr_s[0, blocks].reshape(rows, hidden), wg[...], 1, 1))
        dy = xr_s[1, blocks].reshape(rows, hidden).astype(F32) * loss_scale
        mixed, d_slot = 0.0, 0.0
        for l in range(local_experts):
            here = lane_e == (q * GROUP + row_dev) * local_experts + l
            h = h_in[blocks, l * per:(l + 1) * per, :].reshape(rows, hidden).astype(F32)
            mixed += jnp.sum(jnp.where(here, slot_probs, 0.0), axis=1, keepdims=True) * h
            d_slot += jnp.where(here, jnp.sum(dy * h, axis=1, keepdims=True), 0.0)
        m3 = jnp.concatenate(split3(mixed), axis=0)
        d3 = jnp.concatenate(split3(d_slot), axis=1)

        @pl.loop(0, stages)
        def _(c):
            p = pick[span(q), span(c)]
            big[span(c), :] += dot(jnp.concatenate([p, p, p], axis=0), m3, 0, 0)
            d_acc[span(c), :] += dot(p, d3, 0, 0)

    acc[pl.ds(0, 8), pl.ds(0, LANES)] = jnp.zeros((8, LANES), F32)
    big_g = acc.at[pl.ds(64, experts), :]
    big_g[...] = jnp.zeros((experts, hidden), F32)

    @pl.loop(0, stages)
    def _(c):
        y = big[span(c), :].astype(BF16)
        out_st[span(c), :] = y
        lost = jnp.sum(y.astype(F32) * xr_v[1, span(c), :].astype(F32), axis=0, keepdims=True)
        acc[pl.ds(0, 1), pl.ds(0, LANES)] += jnp.broadcast_to(jnp.sum(lost, axis=1, keepdims=True), (1, LANES))
        d3 = d_acc[span(c), :]
        d_probs = d3[:, :experts] + d3[:, experts:2 * experts] + d3[:, 2 * experts:]
        probs = s_own[span(c), :]
        dl = (probs * (d_probs - jnp.sum(probs * d_probs, axis=1, keepdims=True))).astype(BF16)
        dlog[span(c), :] = dl
        big_g[...] += dot(dl, xr_v[0, span(c), :], 0, 0)
    y_dma = pltpu.make_async_copy(out_st, y_out, out_sem.at[2])

    wide = hidden // 2
    lost = jnp.broadcast_to(acc[pl.ds(0, 1), pl.ds(0, LANES)], (8, LANES)) * loss_scale
    for c in range(half):
        red_s[c, :, :wide] = big_g[8 * (c // 2):8 * (c // 2) + 8, wide * (c % 2):wide * (c % 2) + wide]
        red_s[c, :, wide:] = lost
    mine = me % half
    red_in[mine] = red_s[mine]

    @pl.loop(0, stages)
    def _(c):
        big[span(c), :] = xr_v[1, span(c), :].astype(F32) * loss_scale + dot(dlog[span(c), :], wg[...], 1, 0)
    y_dma.start()

    @pl.loop(half, n - 1)
    def _(p):
        d = peer(p)
        remote(red_s.at[d % half], red_in.at[mine], red_ss, red_rs, d).start()
    send_g(local_experts - 1, 0, 0, GROUP)

    def add_g(l, i):
        await_group(lambda b: g_in.at[l, b], g_rs.at[l * stages + i], i)
        q = group(i)
        g = g_in[l, pl.ds(q * GROUP, GROUP)].reshape(rows, hidden)

        @pl.loop(0, stages)
        def _(c):
            big[span(c), :] += dot(pick[span(q), span(c)], g, 0, 0)

    @pl.loop(0, (local_experts - 1) * stages)
    def _(s):
        add_g(s // stages, s % stages)

    some = pl.ds(0, half - 1)
    red = remote(red_s.at[some], red_in.at[some], red_ss, red_rs, me)
    red.wait_recv()
    swap_s[...] = jnp.sum(red_in[...], axis=0)
    last = local_experts - 1

    @pl.loop(2, stages)
    def _(i):
        send_g(last, i, 0, GROUP)
    swap = remote(swap_s, swap_in, swap_ss, swap_rs, peer(half - 1))
    swap.start()
    send_g(last, 1, 0, GROUP // 2)
    swap.wait_recv()
    full = swap_s[...] + swap_in[...]
    loss_out[...] = full[:, wide:]
    all_s[...] = full[:, :wide]
    all_in[mine] = full[:, :wide]

    @pl.loop(2, stages)
    def _(i):
        add_g(last, i)

    @pl.loop(half, n - 1)
    def _(p):
        remote(all_s, all_in.at[mine], all_ss, all_rs, peer(p)).start()
    send_g(last, 1, GROUP // 2, GROUP)
    add_g(last, 0)
    gathered = remote(all_in.at[some], all_in.at[some], all_ss, all_rs, me)
    gathered.wait_recv()
    for c in range(half):
        gg_out[8 * (c // 2):8 * (c // 2) + 8, wide * (c % 2):wide * (c % 2) + wide] = all_in[c]
    y_dma.wait()
    add_g(last, 1)

    @pl.loop(0, stages)
    def _(c):
        out_st[span(c), :] = big[span(c), :].astype(BF16)
    gx_dma = pltpu.make_async_copy(out_st, gx_out, out_sem.at[3])
    swap.wait_send()
    red.wait_send()
    gathered.wait_send()
    all_h.wait_send()
    for w in range(2):
        remote(xr_s.at[w, most], xr_in.at[w, most], xr_ss, xr_rs.at[0], me).wait_send()
    for l in range(local_experts):
        remote(gs.at[l, most], g_in.at[l, most], g_ss, g_rs.at[0], me).wait_send()
    gx_dma.start()
    pltpu.make_async_copy(w1_v, gu_out, out_sem.at[0]).wait()
    pltpu.make_async_copy(w2_v, gd_out, out_sem.at[1]).wait()
    gx_dma.wait()


def solution(mesh):
    n = mesh.shape['ep']

    def device_step(x, gate_w, up_w, down_w, expert_picks, loss_w):
        tok, hidden = x.shape
        local_experts, capacity = expert_picks.shape
        per = capacity // n
        experts = gate_w.shape[1]
        loss_scale = 1.0 / math.sqrt(tok * n * hidden)
        rows = GROUP * per
        half = n // 2
        hbm = pl.BlockSpec(memory_space=pl.ANY)
        vmem = pl.BlockSpec(memory_space=pltpu.VMEM)
        dma = pltpu.SemaphoreType.DMA
        blocks = (n, per, hidden)
        wide = (n, local_experts * per, hidden)
        chunk = (8, hidden // 2)
        flat = jax.ShapeDtypeStruct(x.shape, BF16)
        y, grad_x, grad_up, grad_down, grad_gate, loss = pl.pallas_call(
            functools.partial(moe_kernel, n, loss_scale),
            out_shape=[flat, flat, jax.ShapeDtypeStruct(up_w.shape, BF16), jax.ShapeDtypeStruct(down_w.shape, BF16),
                       jax.ShapeDtypeStruct((experts, hidden), F32), jax.ShapeDtypeStruct((8, LANES), F32)],
            in_specs=[vmem, hbm, hbm, vmem, hbm, hbm],
            out_specs=[hbm] * 4 + [vmem] * 2,
            scratch_shapes=[
                pltpu.VMEM((2, tok, hidden), BF16), pltpu.VMEM(up_w.shape, BF16), pltpu.VMEM(down_w.shape, BF16),
                pltpu.VMEM((capacity, tok), BF16), pltpu.VMEM((2,) + blocks, BF16), pltpu.VMEM((2,) + blocks, BF16),
                pltpu.VMEM(wide, BF16), pltpu.VMEM(wide, BF16),
                pltpu.VMEM((local_experts,) + blocks, BF16), pltpu.VMEM((local_experts,) + blocks, BF16),
                pltpu.VMEM((capacity, hidden), BF16), pltpu.VMEM((capacity, experts), F32), pltpu.VMEM((tok, experts), F32),
                pltpu.VMEM((capacity, TILE), BF16), pltpu.VMEM((capacity, TILE), BF16),
                pltpu.VMEM((rows, hidden), F32), pltpu.VMEM((capacity, hidden), F32), pltpu.VMEM((tok, hidden), BF16),
                pltpu.VMEM((n, 1, LANES), jnp.int32), pltpu.VMEM((LANES, LANES), F32),
                pltpu.VMEM((tok, 3 * experts), F32), pltpu.VMEM((tok, experts), BF16),
                pltpu.VMEM((half, 8, hidden // 2 + LANES), F32), pltpu.VMEM((half, 8, hidden // 2 + LANES), F32),
                pltpu.VMEM((8, hidden // 2 + LANES), F32), pltpu.VMEM((8, hidden // 2 + LANES), F32),
                pltpu.VMEM(chunk, F32), pltpu.VMEM((half,) + chunk, F32),
                dma((4,)), dma, dma, dma, dma((2 * n // GROUP,)), dma, dma, dma, dma((local_experts * n // GROUP,)),
                dma, dma, dma, dma, dma, dma, dma((4,))],
            compiler_params=pltpu.CompilerParams(collective_id=0, has_side_effects=True, vmem_limit_bytes=63 * 1024 * 1024),
            name='moe',
        )(expert_picks[0].reshape(-1, 1, LANES), x, loss_w, gate_w.T, up_w, down_w)
        return y, loss[0, 0], grad_x, grad_up, grad_down, grad_gate.T

    return jax.shard_map(device_step, mesh=mesh,
                         in_specs=(P('ep'), P(), P('ep'), P('ep'), P('ep'), P('ep')),
                         out_specs=(P('ep'), P(), P('ep'), P('ep'), P('ep'), P()),
                         check_vma=False)
```

time: 629 us -> 280 us (0.45)
  Pallas kernels: 0 us -> 251 us
  blocking collectives: 163 us -> 0 us
  waiting for transfers between devices: 163 us -> 0 us
  matrix products: 125 us -> 0 us
  other arithmetic: 71.2 us -> 0 us
  local copies, waits for them, and re-layouts: 63.8 us -> 24.8 us
  starting transfers between devices: 18.8 us -> 0 us
  between operations: 16.6 us -> 0.64 us
    pallas_call x0 -> x1, Pallas kernels: none -> 251 us  [device_step(): pl.pallas_call(functools.partial(moe_kernel, n, loss_scale), out_shape=[f...]
    dot_general x9 -> x0, matrix products: 125 us -> none  [the longest x1 30.1 us: device_step(): jnp.einsum('lch,lfh->lcf', grad_out_in, down_w, preferred_element_type=jn...]
    all_to_all x4 -> x0, waiting for transfers between devices: 99.6 us -> none  [the longest x1 54.1 us: device_step(): lax.all_to_all(expert_out.reshape(local_experts, group_size, shard_picks,...]
    psum x1 -> x0, blocking collectives: 89 us -> none  [device_step(): lax.psum(jnp.sum(y.astype(jnp.float32) * weight_f32), 'ep') * loss_scale]
    all_to_all x1 -> x0, blocking collectives: 74.4 us -> none  [device_step(): lax.all_to_all(x[asked_ids], 'ep', 1, 1, tiled=True)]
    psum x1 -> x0, waiting for transfers between devices: 63.1 us -> none  [device_step(): lax.psum(lax.dot_general(x, grad_logits, (((0,), (0,)), ((), ())), prefer...]
    gather x6 -> x0, local copies, waits for them, and re-layouts: 38 us -> none  [the longest x3 18.3 us: device_step(): gate_vals = gate_probs[asked_ids, expert_col]]
    scatter-add x2 -> x0, other arithmetic: 31.3 us -> none  [the longest x1 15.6 us: device_step(): jax.ops.segment_sum((gate_vals[..., None] * out_back).reshape(-1, hidden)...]
  transfers between devices with their start and end apart: 5 -> 0, of which waited for: 4 -> 0; matrix products, arithmetic and copies ran while one was open for 19% -> 0% of each run, Pallas kernels for 0% -> 0%
where the time goes in v2:
time: 280 us; the launch traced here: 276 us
  Pallas kernels  251 us (90%)
  local copies, waits for them, and re-layouts  24.8 us (9%)
    pallas_call x1, Pallas kernels, device_step(): pl.pallas_call(functools.partial(moe_kernel, n, loss_scale), out_shape=[f...  251 us
    unnamed x7, local copies, waits for them, and re-layouts  22.3 us

profile of v2, /device:TPU:0, one launch (start us, length us, event | category | flops | bytes accessed | tf_op | source)
XLA Modules:
  0.0 276.0 jit_solution(5556415742802265100)
XLA Ops:
  0.6 1.3 slice_bitcast_fusion.ids
  1.9 250.6 %moe.1 = (bf16[1024,768]{1,0:T(8,128)(2,1)}, bf16[1024,768]{1,0:T(8,128)(2,1)}, bf16[2,768,3072]{2,1,0:T(8,128)(2,1)}, bf16[2,3072,768]{2,1,0:T(8,128)(2,1)}, f32[64,768]{1,0:T(8,128)}, /*index=5*/f32[8,128]{1,0:T(8,128)}) custom-call(s32[8,1,128]{2,1,0:T(1,128)} %slice_bitcast_fusion.ids, bf16[1024,768]{1,0:T(8,128)(2,1)} %x.1, bf16[1024,768]{1,0:T(8,128)(2,1)} %r.1, ...), custom_call_target="tpu_custom_call" | custom-call | tf_op jit(solution)/shard_map/moe/pallas_call | solution.py:415
  252.5 1.2 slice.7
  253.7 2.7 copy.17
  256.4 2.7 copy.18
  259.0 8.3 %copy.19 = bf16[2,768,3072]{2,1,0:T(8,128)(2,1)} copy(bf16[2,768,3072]{2,1,0:T(8,128)(2,1)} %get-tuple-element.27) | data formatting | bytes 18874368
  267.3 0.0 copy-start
  267.3 8.1 %copy.20 = bf16[2,3072,768]{2,1,0:T(8,128)(2,1)} copy(bf16[2,3072,768]{2,1,0:T(8,128)(2,1)} %get-tuple-element.28) | data formatting | bytes 18874368
  275.3 0.0 copy-done
  275.3 0.7 copy.21
Async XLA Ops:
  267.3 8.1 %copy-start = (f32[64,768]{1,0:T(8,128)S(1)}, f32[64,768]{1,0:T(8,128)}, u32[]{:S(2)}) copy-start(f32[64,768]{1,0:T(8,128)} %get-tuple-element.17) | copy-start | bytes 589828

commit v3 on v2

--- a/solution.py
+++ b/solution.py
@@ -37,10 +37,10 @@
 
 
 def moe_kernel(n, loss_scale, ids, x, r, wg, w1, w2,
-               y_out, gx_out, gu_out, gd_out, gg_out, loss_out,
-               xr_v, w1_v, w2_v, pick, xr_s, xr_in, hs, h_in, gs, g_in, dh_v, s_in, s_own, u_t, da_t, acc, big, out_st,
+               y_out, gx_out, w1_v, w2_v, gg_out, loss_out, u_far, da_far,
+               xr_v, pick, xr_s, xr_in, hs, h_in, gs, g_in, dh_v, s_in, s_own, u_t, da_t, acc, big,
                ids_in, ids_t, d_acc, dlog, red_s, red_in, swap_s, swap_in, all_s, all_in,
-               load_sem, ids_ss, ids_rs, xr_ss, xr_rs, h_ss, h_rs, g_ss, g_rs, red_ss, red_rs, swap_ss, swap_rs, all_ss, all_rs, out_sem):
+               load_sem, ids_ss, ids_rs, xr_ss, xr_rs, h_ss, h_rs, g_ss, g_rs, red_ss, red_rs, swap_ss, swap_rs, all_ss, all_rs, put_sem, get_sem):
     me = lax.axis_index('ep')
     bits = n.bit_length() - 1
     stages = n // GROUP
@@ -173,7 +173,7 @@
         def _(l):
             acc[...] = jnp.zeros_like(acc)
 
-            @pl.loop(0, tiles)
+            @pl.loop(0, tiles, unroll=2)
             def _(t):
                 at = pl.ds(pl.multiple_of(t * TILE, TILE), TILE)
                 a = dot(xg, w1_v[l, :, at])
@@ -206,14 +206,10 @@
             def _():
                 g_in[l, me] = gs[l, me]
 
-    def grads_out(step):
-        l, t = step // tiles, step % tiles
-        at = pl.ds(pl.multiple_of(t * TILE, TILE), TILE)
-        pltpu.make_async_copy(w1_v.at[l, :, at], gu_out.at[l, :, at], out_sem.at[0]).start()
-        pltpu.make_async_copy(w2_v.at[l, at, :], gd_out.at[l, at, :], out_sem.at[1]).start()
-
-    @pl.loop(0, local_experts)
-    def _(l):
+    def tile_at(t):
+        return pl.ds(pl.multiple_of(t * TILE, TILE), TILE)
+
+    def start_rows(l):
         @pl.loop(0, stages)
         def _(q):
             gate = jnp.sum(jnp.where(lane_e == me * local_experts + l, s_in[span(q), :], 0.0), axis=1, keepdims=True)
@@ -221,48 +217,85 @@
             dh_v[span(q), :] = (gate * dy).astype(BF16)
             big[span(q), :] = jnp.zeros((rows, hidden), F32)
 
-        @pl.loop(0, tiles)
-        def _(t):
-            step = l * tiles + t
-            at = pl.ds(pl.multiple_of(t * TILE, TILE), TILE)
-
-            @pl.loop(0, stages)
-            def _(q):
-                up = w1_v[l, :, at]
-                a = dot(xr_in[0, pl.ds(q * GROUP, GROUP)].reshape(rows, hidden), up)
-                th = jnp.tanh(C0 * (a + C1 * (a * a * a)))
-                side = 0.5 * (1.0 + th)
-                u_t[span(q), :] = (a * side).astype(BF16)
-                slope = side + 0.5 * a * (1.0 - th * th) * (C0 + (3.0 * C0 * C1) * (a * a))
-                du = dot(dh_v[span(q), :], w2_v[l, at, :], 1, 1).astype(BF16).astype(F32)
-                da = (slope * du).astype(BF16)
-                da_t[span(q), :] = da
-                big[span(q), :] += dot(da, up, 1, 1)
-
-            @pl.when(step > 0)
-            def _():
-                grads_out(step - 1)
-
-            @pl.loop(0, TILE // rows)
-            def _(m):
-                part = dot(u_t[:, span(m)], dh_v[...], 0, 0).astype(BF16)
-                w2_v[l, pl.ds(pl.multiple_of(t * TILE + m * rows, rows), rows), :] = part
-
-            @pl.loop(0, hidden // rows)
-            def _(m):
-                xm = xr_in[0, :, :, span(m)].reshape(tok, rows)
-                w1_v[l, span(m), at] = dot(xm, da_t[...], 0, 0).astype(BF16)
-
+    def row_grads(l, t, slot):
+        at = tile_at(t)
+
+        @pl.loop(0, stages, unroll=2)
+        def _(q):
+            up = w1_v[l, :, at]
+            a = dot(xr_in[0, pl.ds(q * GROUP, GROUP)].reshape(rows, hidden), up)
+            th = jnp.tanh(C0 * (a + C1 * (a * a * a)))
+            side = 0.5 * (1.0 + th)
+            u_t[slot, span(q), :] = (a * side).astype(BF16)
+            slope = side + 0.5 * a * (1.0 - th * th) * (C0 + (3.0 * C0 * C1) * (a * a))
+            du = dot(dh_v[span(q), :], w2_v[l, at, :], 1, 1).astype(BF16).astype(F32)
+            da = (slope * du).astype(BF16)
+            da_t[slot, span(q), :] = da
+            big[span(q), :] += dot(da, up, 1, 1)
+
+    def weight_grads(l, t, slot):
+        at = tile_at(t)
+
+        @pl.loop(0, TILE // rows)
+        def _(m):
+            part = dot(u_t[slot, :, span(m)], dh_v[...], 0, 0).astype(BF16)
+            w2_v[l, pl.ds(pl.multiple_of(t * TILE + m * rows, rows), rows), :] = part
+
+        @pl.loop(0, hidden // rows)
+        def _(m):
+            xm = xr_in[0, :, :, span(m)].reshape(tok, rows)
+            w1_v[l, span(m), at] = dot(xm, da_t[slot], 0, 0).astype(BF16)
+
+    def finish_rows(l):
         @pl.loop(0, stages)
         def _(q):
             gs[l, pl.ds(q * GROUP, GROUP)] = big[span(q), :].astype(BF16).reshape(GROUP, per, hidden)
 
-        @pl.when(l < local_experts - 1)
-        def _():
-            @pl.loop(0, stages)
-            def _(i):
-                send_g(l, i, 0, GROUP)
-    grads_out(local_experts * tiles - 1)
+    last = local_experts - 1
+
+    @pl.loop(0, last)
+    def _(l):
+        start_rows(l)
+
+        @pl.loop(0, tiles)
+        def _(t):
+            row_grads(l, t, 0)
+            weight_grads(l, t, 0)
+        finish_rows(l)
+
+        @pl.loop(0, stages)
+        def _(i):
+            send_g(l, i, 0, GROUP)
+
+    def aside(t, slot):
+        return (pltpu.make_async_copy(u_t.at[slot], u_far.at[t], put_sem.at[slot]),
+                pltpu.make_async_copy(da_t.at[slot], da_far.at[t], put_sem.at[2 + slot]))
+
+    def fetch(t, slot):
+        return (pltpu.make_async_copy(u_far.at[t], u_t.at[slot], get_sem.at[slot]),
+                pltpu.make_async_copy(da_far.at[t], da_t.at[slot], get_sem.at[2 + slot]))
+
+    start_rows(last)
+
+    @pl.loop(0, tiles)
+    def _(t):
+        slot = t % 2
+
+        @pl.when(t >= 2)
+        def _():
+            for c in aside(t - 2, slot):
+                c.wait()
+        row_grads(last, t, slot)
+
+        @pl.when(t < tiles - 2)
+        def _():
+            for c in aside(t, slot):
+                c.start()
+    finish_rows(last)
+    for slot in range(2):
+        weight_grads(last, tiles - 2 + slot, slot)
+        for c in fetch(slot, slot):
+            c.start()
 
     all_h = remote(hs.at[most], h_in.at[most], h_ss, h_rs, me)
     all_h.wait_recv()
@@ -299,7 +332,7 @@
     @pl.loop(0, stages)
     def _(c):
         y = big[span(c), :].astype(BF16)
-        out_st[span(c), :] = y
+        y_out[span(c), :] = y
         lost = jnp.sum(y.astype(F32) * xr_v[1, span(c), :].astype(F32), axis=0, keepdims=True)
         acc[pl.ds(0, 1), pl.ds(0, LANES)] += jnp.broadcast_to(jnp.sum(lost, axis=1, keepdims=True), (1, LANES))
         d3 = d_acc[span(c), :]
@@ -308,7 +341,6 @@
         dl = (probs * (d_probs - jnp.sum(probs * d_probs, axis=1, keepdims=True))).astype(BF16)
         dlog[span(c), :] = dl
         big_g[...] += dot(dl, xr_v[0, span(c), :], 0, 0)
-    y_dma = pltpu.make_async_copy(out_st, y_out, out_sem.at[2])
 
     wide = hidden // 2
     lost = jnp.broadcast_to(acc[pl.ds(0, 1), pl.ds(0, LANES)], (8, LANES)) * loss_scale
@@ -321,13 +353,27 @@
     @pl.loop(0, stages)
     def _(c):
         big[span(c), :] = xr_v[1, span(c), :].astype(F32) * loss_scale + dot(dlog[span(c), :], wg[...], 1, 0)
-    y_dma.start()
 
     @pl.loop(half, n - 1)
     def _(p):
         d = peer(p)
         remote(red_s.at[d % half], red_in.at[mine], red_ss, red_rs, d).start()
-    send_g(local_experts - 1, 0, 0, GROUP)
+    @pl.loop(2, stages)
+    def _(i):
+        send_g(last, i, 0, GROUP)
+    send_g(last, 0, 0, GROUP)
+
+    @pl.loop(0, tiles - 2)
+    def _(t):
+        slot = t % 2
+        for c in fetch(t, slot):
+            c.wait()
+        weight_grads(last, t, slot)
+
+        @pl.when(t < tiles - 4)
+        def _():
+            for c in fetch(t + 2, slot):
+                c.start()
 
     def add_g(l, i):
         await_group(lambda b: g_in.at[l, b], g_rs.at[l * stages + i], i)
@@ -338,7 +384,7 @@
         def _(c):
             big[span(c), :] += dot(pick[span(q), span(c)], g, 0, 0)
 
-    @pl.loop(0, (local_experts - 1) * stages)
+    @pl.loop(0, last * stages - 1)
     def _(s):
         add_g(s // stages, s % stages)
 
@@ -346,40 +392,31 @@
     red = remote(red_s.at[some], red_in.at[some], red_ss, red_rs, me)
     red.wait_recv()
     swap_s[...] = jnp.sum(red_in[...], axis=0)
-    last = local_experts - 1
-
-    @pl.loop(2, stages)
-    def _(i):
-        send_g(last, i, 0, GROUP)
+    add_g(last - 1, stages - 1)
     swap = remote(swap_s, swap_in, swap_ss, swap_rs, peer(half - 1))
     swap.start()
-    send_g(last, 1, 0, GROUP // 2)
+    send_g(last, 1, 0, GROUP)
+    add_g(last, 2)
     swap.wait_recv()
     full = swap_s[...] + swap_in[...]
     loss_out[...] = full[:, wide:]
     all_s[...] = full[:, :wide]
     all_in[mine] = full[:, :wide]
-
-    @pl.loop(2, stages)
-    def _(i):
-        add_g(last, i)
+    add_g(last, 3)
 
     @pl.loop(half, n - 1)
     def _(p):
         remote(all_s, all_in.at[mine], all_ss, all_rs, peer(p)).start()
-    send_g(last, 1, GROUP // 2, GROUP)
     add_g(last, 0)
+    add_g(last, 1)
+
+    @pl.loop(0, stages)
+    def _(c):
+        gx_out[span(c), :] = big[span(c), :].astype(BF16)
     gathered = remote(all_in.at[some], all_in.at[some], all_ss, all_rs, me)
     gathered.wait_recv()
     for c in range(half):
         gg_out[8 * (c // 2):8 * (c // 2) + 8, wide * (c % 2):wide * (c % 2) + wide] = all_in[c]
-    y_dma.wait()
-    add_g(last, 1)
-
-    @pl.loop(0, stages)
-    def _(c):
-        out_st[span(c), :] = big[span(c), :].astype(BF16)
-    gx_dma = pltpu.make_async_copy(out_st, gx_out, out_sem.at[3])
     swap.wait_send()
     red.wait_send()
     gathered.wait_send()
@@ -388,10 +425,6 @@
         remote(xr_s.at[w, most], xr_in.at[w, most], xr_ss, xr_rs.at[0], me).wait_send()
     for l in range(local_experts):
         remote(gs.at[l, most], g_in.at[l, most], g_ss, g_rs.at[0], me).wait_send()
-    gx_dma.start()
-    pltpu.make_async_copy(w1_v, gu_out, out_sem.at[0]).wait()
-    pltpu.make_async_copy(w2_v, gd_out, out_sem.at[1]).wait()
-    gx_dma.wait()
 
 
 def solution(mesh):
@@ -411,29 +444,30 @@
         blocks = (n, per, hidden)
         wide = (n, local_experts * per, hidden)
         chunk = (8, hidden // 2)
-        flat = jax.ShapeDtypeStruct(x.shape, BF16)
-        y, grad_x, grad_up, grad_down, grad_gate, loss = pl.pallas_call(
+        flat = pltpu.VMEM(x.shape, BF16)
+        aside = jax.ShapeDtypeStruct((up_w.shape[2] // TILE, capacity, TILE), BF16)
+        y, grad_x, grad_up, grad_down, grad_gate, loss, _, _ = pl.pallas_call(
             functools.partial(moe_kernel, n, loss_scale),
-            out_shape=[flat, flat, jax.ShapeDtypeStruct(up_w.shape, BF16), jax.ShapeDtypeStruct(down_w.shape, BF16),
-                       jax.ShapeDtypeStruct((experts, hidden), F32), jax.ShapeDtypeStruct((8, LANES), F32)],
+            out_shape=[flat, flat, pltpu.VMEM(up_w.shape, BF16), pltpu.VMEM(down_w.shape, BF16),
+                       jax.ShapeDtypeStruct((experts, hidden), F32), jax.ShapeDtypeStruct((8, LANES), F32)] + [aside] * 2,
             in_specs=[vmem, hbm, hbm, vmem, hbm, hbm],
-            out_specs=[hbm] * 4 + [vmem] * 2,
+            out_specs=[vmem] * 6 + [hbm] * 2,
             scratch_shapes=[
-                pltpu.VMEM((2, tok, hidden), BF16), pltpu.VMEM(up_w.shape, BF16), pltpu.VMEM(down_w.shape, BF16),
+                pltpu.VMEM((2, tok, hidden), BF16),
                 pltpu.VMEM((capacity, tok), BF16), pltpu.VMEM((2,) + blocks, BF16), pltpu.VMEM((2,) + blocks, BF16),
                 pltpu.VMEM(wide, BF16), pltpu.VMEM(wide, BF16),
                 pltpu.VMEM((local_experts,) + blocks, BF16), pltpu.VMEM((local_experts,) + blocks, BF16),
                 pltpu.VMEM((capacity, hidden), BF16), pltpu.VMEM((capacity, experts), F32), pltpu.VMEM((tok, experts), F32),
-                pltpu.VMEM((capacity, TILE), BF16), pltpu.VMEM((capacity, TILE), BF16),
-                pltpu.VMEM((rows, hidden), F32), pltpu.VMEM((capacity, hidden), F32), pltpu.VMEM((tok, hidden), BF16),
+                pltpu.VMEM((2, capacity, TILE), BF16), pltpu.VMEM((2, capacity, TILE), BF16),
+                pltpu.VMEM((rows, hidden), F32), pltpu.VMEM((capacity, hidden), F32),
                 pltpu.VMEM((n, 1, LANES), jnp.int32), pltpu.VMEM((LANES, LANES), F32),
                 pltpu.VMEM((tok, 3 * experts), F32), pltpu.VMEM((tok, experts), BF16),
                 pltpu.VMEM((half, 8, hidden // 2 + LANES), F32), pltpu.VMEM((half, 8, hidden // 2 + LANES), F32),
                 pltpu.VMEM((8, hidden // 2 + LANES), F32), pltpu.VMEM((8, hidden // 2 + LANES), F32),
                 pltpu.VMEM(chunk, F32), pltpu.VMEM((half,) + chunk, F32),
                 dma((4,)), dma, dma, dma, dma((2 * n // GROUP,)), dma, dma, dma, dma((local_experts * n // GROUP,)),
-                dma, dma, dma, dma, dma, dma, dma((4,))],
-            compiler_params=pltpu.CompilerParams(collective_id=0, has_side_effects=True, vmem_limit_bytes=63 * 1024 * 1024),
+                dma, dma, dma, dma, dma, dma, dma((4,)), dma((4,))],
+            compiler_params=pltpu.CompilerParams(collective_id=0, has_side_effects=True, vmem_limit_bytes=41 * 1024 * 1024),
             name='moe',
         )(expert_picks[0].reshape(-1, 1, LANES), x, loss_w, gate_w.T, up_w, down_w)
         return y, loss[0, 0], grad_x, grad_up, grad_down, grad_gate.T

time: 280 us -> 250 us (0.89); the launches traced: 276 us -> 250 us
  Pallas kernels: 251 us -> 236 us
  local copies, waits for them, and re-layouts: 24.8 us -> 12.9 us
    pallas_call x1, Pallas kernels: 251 us -> 236 us  [device_step(): pl.pallas_call(functools.partial(moe_kernel, n, loss_scale), out_shape=[f...]
    unnamed x7, local copies, waits for them, and re-layouts: 22.3 us -> 10.4 us
where the time goes in v3:
time: 250 us
  Pallas kernels  236 us (94%)
  local copies, waits for them, and re-layouts  12.9 us (5%)
    pallas_call x1, Pallas kernels, device_step(): pl.pallas_call(functools.partial(moe_kernel, n, loss_scale), out_shape=[f...  236 us
    unnamed x7, local copies, waits for them, and re-layouts  10.4 us

profile of v3, /device:TPU:0, one launch (start us, length us, event | category | flops | bytes accessed | tf_op | source)
XLA Modules:
  0.0 250.0 jit_solution(15207943599063431547)
XLA Ops:
  0.6 1.3 slice_bitcast_fusion.ids
  1.9 236.4 %moe.1 = (bf16[1024,768]{1,0:T(8,128)(2,1)S(1)}, bf16[1024,768]{1,0:T(8,128)(2,1)S(1)}, bf16[2,768,3072]{2,1,0:T(8,128)(2,1)S(1)}, bf16[2,3072,768]{2,1,0:T(8,12...) custom-call(s32[8,1,128]{2,1,0:T(1,128)} %slice_bitcast_fusion.ids, ...), custom_call_target="tpu_custom_call" | custom-call | tf_op jit(solution)/shard_map/moe/pallas_call | solution.py:449
  238.4 1.2 slice.7
  239.6 1.1 copy.17
  240.7 1.1 copy.18
  241.8 3.7 %copy.19 = bf16[2,768,3072]{2,1,0:T(8,128)(2,1)} copy(bf16[2,768,3072]{2,1,0:T(8,128)(2,1)S(1)} %get-tuple-element.21) | data formatting | bytes 18874368
  245.6 0.0 copy-start
  245.6 3.7 %copy.20 = bf16[2,3072,768]{2,1,0:T(8,128)(2,1)} copy(bf16[2,3072,768]{2,1,0:T(8,128)(2,1)S(1)} %get-tuple-element.22) | data formatting | bytes 18874368
  249.3 0.0 copy-done
  249.3 0.7 copy.21
Async XLA Ops:
  245.6 3.7 %copy-start = (f32[64,768]{1,0:T(8,128)S(1)}, f32[64,768]{1,0:T(8,128)}, u32[]{:S(2)}) copy-start(f32[64,768]{1,0:T(8,128)} %get-tuple-element.17) | copy-start | bytes 589828

commit v4 on v3

--- a/solution.py
+++ b/solution.py
@@ -36,9 +36,9 @@
     return sum(((a // (1 << i) + b // (1 << i)) % 2) * (1 << i) for i in range(bits))
 
 
-def moe_kernel(n, loss_scale, ids, x, r, wg, w1, w2,
+def moe_kernel(n, loss_scale, picks, x, r, gate_w, w1, w2,
                y_out, gx_out, w1_v, w2_v, gg_out, loss_out, u_far, da_far,
-               xr_v, pick, xr_s, xr_in, hs, h_in, gs, g_in, dh_v, s_in, s_own, u_t, da_t, acc, big,
+               picks_v, ids, wg, xr_v, pick, xr_s, xr_in, hs, h_in, gs, g_in, dh_v, s_in, s_own, u_t, da_t, acc, big,
                ids_in, ids_t, d_acc, dlog, red_s, red_in, swap_s, swap_in, all_s, all_in,
                load_sem, ids_ss, ids_rs, xr_ss, xr_rs, h_ss, h_rs, g_ss, g_rs, red_ss, red_rs, swap_ss, swap_rs, all_ss, all_rs, put_sem, get_sem):
     me = lax.axis_index('ep')
@@ -51,6 +51,7 @@
     local_experts, _, ffn = w1_v.shape
     tiles = ffn // TILE
     experts = wg.shape[0]
+    packed = LANES // per
     most = pl.ds(0, n - 1)
 
     def peer(p):
@@ -65,7 +66,8 @@
     def span(q):
         return pl.ds(pl.multiple_of(q * rows, rows), rows)
 
-    loads = [pltpu.make_async_copy(x, xr_v.at[0], load_sem.at[0]), pltpu.make_async_copy(r, xr_v.at[1], load_sem.at[1]),
+    loads = [pltpu.make_async_copy(picks, picks_v, load_sem.at[4]), pltpu.make_async_copy(gate_w, wg, load_sem.at[5]),
+             pltpu.make_async_copy(x, xr_v.at[0], load_sem.at[0]), pltpu.make_async_copy(r, xr_v.at[1], load_sem.at[1]),
              pltpu.make_async_copy(w1, w1_v, load_sem.at[2]), pltpu.make_async_copy(w2, w2_v, load_sem.at[3])]
     for c in loads:
         c.start()
@@ -75,9 +77,11 @@
     @pl.loop(0, n - 1)
     def _(p):
         pl.semaphore_signal(barrier, inc=1, device_id=(peer(p),), device_id_type=pl.DeviceIdType.MESH)
+
+    loads[0].wait()
+    for c in range(n // packed):
+        ids[c] = picks_v[0:1, c * LANES:(c + 1) * LANES]
     pl.semaphore_wait(barrier, n - 1)
-
-    packed = LANES // per
 
     @pl.loop(0, n - 1)
     def _(p):
@@ -93,46 +97,64 @@
     lane = lax.broadcasted_iota(jnp.int32, (per, LANES), 1)
     tok_iota = (lax.broadcasted_iota(jnp.int32, (per, tok), 1) + me * tok).astype(F32)
 
-    loads[0].wait()
-    loads[1].wait()
-
-    @pl.loop(0, 2 * stages + 1)
+    for c in loads[1:4]:
+        c.wait()
+
+    def send_rows(s):
+        w, i = s // stages, s % stages
+
+        @pl.loop(0, GROUP)
+        def _(j):
+            p = i * GROUP + j
+
+            @pl.when(p < n - 1)
+            def _():
+                d = peer(p)
+                remote(xr_s.at[w, d], xr_in.at[w, me], xr_ss, xr_rs.at[s], d).start()
+
+            @pl.when(p == n - 1)
+            def _():
+                xr_in[w, me] = xr_s[w, me]
+
+    def gather_rows(s):
+        w, q = s // stages, group(s % stages)
+        xr_s[w, pl.ds(q * GROUP, GROUP)] = dot(pick[span(q), :], xr_v[w]).astype(BF16).reshape(GROUP, per, hidden)
+
+    @pl.loop(0, stages)
     def _(s):
-        @pl.when(s < stages)
-        def _():
-            base = group(s % stages) * GROUP
-            for j in range(GROUP):
-                col = jnp.sum(jnp.where(lane == base + j, cols, 0.0), axis=1, keepdims=True)
-                at = pl.multiple_of((base + j) * per, per)
-                pick[pl.ds(at, per), :] = jnp.where(tok_iota == col, 1.0, 0.0).astype(BF16)
-
-        @pl.when(s < 2 * stages)
-        def _():
-            w, q = s // stages, group(s % stages)
-            xr_s[w, pl.ds(q * GROUP, GROUP)] = dot(pick[span(q), :], xr_v[w]).astype(BF16).reshape(GROUP, per, hidden)
+        base = group(s) * GROUP
+        for j in range(GROUP):
+            col = jnp.sum(jnp.where(lane == base + j, cols, 0.0), axis=1, keepdims=True)
+            at = pl.multiple_of((base + j) * per, per)
+            pick[pl.ds(at, per), :] = jnp.where(tok_iota == col, 1.0, 0.0).astype(BF16)
 
         @pl.when(s > 0)
         def _():
-            w, i = (s - 1) // stages, (s - 1) % stages
-
-            @pl.loop(0, GROUP)
-            def _(j):
-                p = i * GROUP + j
-
-                @pl.when(p < n - 1)
-                def _():
-                    d = peer(p)
-                    remote(xr_s.at[w, d], xr_in.at[w, me], xr_ss, xr_rs.at[w * stages + i], d).start()
-
-                @pl.when(p == n - 1)
-                def _():
-                    xr_in[w, me] = xr_s[w, me]
+            send_rows(s - 1)
+        gather_rows(s)
+
+    @pl.loop(stages, 2 * stages)
+    def _(s):
+        gather_rows(s)
+        send_rows(s - 1)
 
     @pl.loop(0, stages)
     def _(c):
         s_own[span(c), :] = softmax(dot(xr_v[0, span(c), :], wg[...], 1, 1))
-    loads[2].wait()
-    loads[3].wait()
+    send_rows(2 * stages - 1)
+    loads[4].wait()
+    loads[5].wait()
+
+    @pl.loop(0, stages * stages)
+    def _(k):
+        q, c = k // stages, k % stages
+
+        @pl.when(c >= q)
+        def _():
+            upper = jnp.transpose(pick[span(q), span(c)].astype(F32)).astype(BF16)
+            lower = jnp.transpose(pick[span(c), span(q)].astype(F32)).astype(BF16)
+            pick[span(q), span(c)] = lower
+            pick[span(c), span(q)] = upper
 
     def await_group(ref, sem, i):
         for cond, size in ((i < stages - 1, GROUP), (i == stages - 1, GROUP - 1)):
@@ -294,6 +316,11 @@
     finish_rows(last)
     for slot in range(2):
         weight_grads(last, tiles - 2 + slot, slot)
+        if slot == 0:
+            @pl.loop(2, stages)
+            def _(i):
+                send_g(last, i, 0, GROUP)
+            send_g(last, 0, 0, GROUP)
         for c in fetch(slot, slot):
             c.start()
 
@@ -321,9 +348,9 @@
 
         @pl.loop(0, stages)
         def _(c):
-            p = pick[span(q), span(c)]
-            big[span(c), :] += dot(jnp.concatenate([p, p, p], axis=0), m3, 0, 0)
-            d_acc[span(c), :] += dot(p, d3, 0, 0)
+            p = pick[span(c), span(q)]
+            big[span(c), :] += dot(jnp.concatenate([p, p, p], axis=1), m3)
+            d_acc[span(c), :] += dot(p, d3)
 
     acc[pl.ds(0, 8), pl.ds(0, LANES)] = jnp.zeros((8, LANES), F32)
     big_g = acc.at[pl.ds(64, experts), :]
@@ -358,10 +385,7 @@
     def _(p):
         d = peer(p)
         remote(red_s.at[d % half], red_in.at[mine], red_ss, red_rs, d).start()
-    @pl.loop(2, stages)
-    def _(i):
-        send_g(last, i, 0, GROUP)
-    send_g(last, 0, 0, GROUP)
+    send_g(last, 1, 0, GROUP // 2)
 
     @pl.loop(0, tiles - 2)
     def _(t):
@@ -382,20 +406,20 @@
 
         @pl.loop(0, stages)
         def _(c):
-            big[span(c), :] += dot(pick[span(q), span(c)], g, 0, 0)
-
-    @pl.loop(0, last * stages - 1)
-    def _(s):
-        add_g(s // stages, s % stages)
+            big[span(c), :] += dot(pick[span(c), span(q)], g)
 
     some = pl.ds(0, half - 1)
     red = remote(red_s.at[some], red_in.at[some], red_ss, red_rs, me)
     red.wait_recv()
     swap_s[...] = jnp.sum(red_in[...], axis=0)
-    add_g(last - 1, stages - 1)
+    add_g(0, 0)
     swap = remote(swap_s, swap_in, swap_ss, swap_rs, peer(half - 1))
     swap.start()
-    send_g(last, 1, 0, GROUP)
+    send_g(last, 1, GROUP // 2, GROUP)
+
+    @pl.loop(1, last * stages)
+    def _(s):
+        add_g(s // stages, s % stages)
     add_g(last, 2)
     swap.wait_recv()
     full = swap_s[...] + swap_in[...]
@@ -425,6 +449,17 @@
         remote(xr_s.at[w, most], xr_in.at[w, most], xr_ss, xr_rs.at[0], me).wait_send()
     for l in range(local_experts):
         remote(gs.at[l, most], g_in.at[l, most], g_ss, g_rs.at[0], me).wait_send()
+
+
+def flush_kernel(y, gx, gu, gd, gg, loss, y_out, gx_out, gu_out, gd_out, gg_out, loss_out, sem):
+    parts = [(gu.at[l], gu_out.at[l]) for l in range(gu.shape[0])] + [(gd.at[l], gd_out.at[l]) for l in range(gd.shape[0])]
+    parts += [(y, y_out), (gx, gx_out), (gg, gg_out)]
+    copies = [pltpu.make_async_copy(a, b, sem.at[k]) for k, (a, b) in enumerate(parts)]
+    for c in copies:
+        c.start()
+    loss_out[0, 0] = loss[0, 0]
+    for c in copies:
+        c.wait()
 
 
 def solution(mesh):
@@ -446,14 +481,15 @@
         chunk = (8, hidden // 2)
         flat = pltpu.VMEM(x.shape, BF16)
         aside = jax.ShapeDtypeStruct((up_w.shape[2] // TILE, capacity, TILE), BF16)
-        y, grad_x, grad_up, grad_down, grad_gate, loss, _, _ = pl.pallas_call(
+        *held, _, _ = pl.pallas_call(
             functools.partial(moe_kernel, n, loss_scale),
             out_shape=[flat, flat, pltpu.VMEM(up_w.shape, BF16), pltpu.VMEM(down_w.shape, BF16),
-                       jax.ShapeDtypeStruct((experts, hidden), F32), jax.ShapeDtypeStruct((8, LANES), F32)] + [aside] * 2,
-            in_specs=[vmem, hbm, hbm, vmem, hbm, hbm],
+                       pltpu.VMEM((experts, hidden), F32), pltpu.VMEM((8, LANES), F32)] + [aside] * 2,
+            in_specs=[hbm] * 6,
             out_specs=[vmem] * 6 + [hbm] * 2,
             scratch_shapes=[
-                pltpu.VMEM((2, tok, hidden), BF16),
+                pltpu.VMEM(expert_picks.shape, jnp.int32), pltpu.VMEM((capacity // LANES, 1, LANES), jnp.int32),
+                pltpu.VMEM((experts, hidden), BF16), pltpu.VMEM((2, tok, hidden), BF16),
                 pltpu.VMEM((capacity, tok), BF16), pltpu.VMEM((2,) + blocks, BF16), pltpu.VMEM((2,) + blocks, BF16),
                 pltpu.VMEM(wide, BF16), pltpu.VMEM(wide, BF16),
                 pltpu.VMEM((local_experts,) + blocks, BF16), pltpu.VMEM((local_experts,) + blocks, BF16),
@@ -465,11 +501,20 @@
                 pltpu.VMEM((half, 8, hidden // 2 + LANES), F32), pltpu.VMEM((half, 8, hidden // 2 + LANES), F32),
                 pltpu.VMEM((8, hidden // 2 + LANES), F32), pltpu.VMEM((8, hidden // 2 + LANES), F32),
                 pltpu.VMEM(chunk, F32), pltpu.VMEM((half,) + chunk, F32),
-                dma((4,)), dma, dma, dma, dma((2 * n // GROUP,)), dma, dma, dma, dma((local_experts * n // GROUP,)),
+                dma((6,)), dma, dma, dma, dma((2 * n // GROUP,)), dma, dma, dma, dma((local_experts * n // GROUP,)),
                 dma, dma, dma, dma, dma, dma, dma((4,)), dma((4,))],
             compiler_params=pltpu.CompilerParams(collective_id=0, has_side_effects=True, vmem_limit_bytes=41 * 1024 * 1024),
             name='moe',
-        )(expert_picks[0].reshape(-1, 1, LANES), x, loss_w, gate_w.T, up_w, down_w)
+        )(expert_picks, x, loss_w, gate_w.T, up_w, down_w)
+        y, grad_x, grad_up, grad_down, grad_gate, loss = pl.pallas_call(
+            flush_kernel,
+            out_shape=[jax.ShapeDtypeStruct(v.shape, v.dtype) for v in held[:5]] + [jax.ShapeDtypeStruct((1, 1), F32)],
+            in_specs=[vmem] * 6,
+            out_specs=[hbm] * 5 + [pl.BlockSpec(memory_space=pltpu.SMEM)],
+            scratch_shapes=[dma((9,))],
+            compiler_params=pltpu.CompilerParams(vmem_limit_bytes=1024 * 1024),
+            name='flush',
+        )(*held)
         return y, loss[0, 0], grad_x, grad_up, grad_down, grad_gate.T
 
     return jax.shard_map(device_step, mesh=mesh,

time: 250 us -> 231 us (0.924)
  local copies, waits for them, and re-layouts: 12.9 us -> 0 us
  Pallas kernels: 236 us -> 230 us
    pallas_call x1, Pallas kernels: 236 us -> 222 us  [device_step(): pl.pallas_call(functools.partial(moe_kernel, n, loss_scale), out_shape=[f...]
    unnamed x7 -> x0, local copies, waits for them, and re-layouts: 10.4 us -> none
    pallas_call x0 -> x1, Pallas kernels: none -> 8.03 us  [device_step(): pl.pallas_call(flush_kernel, out_shape=[jax.ShapeDtypeStruct(v.shape, v.d...]
where the time goes in v4:
time: 231 us
  Pallas kernels  230 us (100%)
    pallas_call x1, Pallas kernels, device_step(): pl.pallas_call(functools.partial(moe_kernel, n, loss_scale), out_shape=[f...  222 us
    pallas_call x1, Pallas kernels, device_step(): pl.pallas_call(flush_kernel, out_shape=[jax.ShapeDtypeStruct(v.shape, v.d...  8.03 us

profile of v4, /device:TPU:0, one launch (start us, length us, event | category | flops | bytes accessed | tf_op | source)
XLA Modules:
  0.0 230.6 jit_solution(7609271104309682580)
XLA Ops:
  0.6 221.9 %moe.1 = (bf16[1024,768]{1,0:T(8,128)(2,1)S(1)}, bf16[1024,768]{1,0:T(8,128)(2,1)S(1)}, bf16[2,768,3072]{2,1,0:T(8,128)(2,1)S(1)}, bf16[2,3072,768]{2,1,0:T(8,12...) custom-call(s32[2,1024]{1,0:T(2,128)} %picks.1, ...), custom_call_target="tpu_custom_call" | custom-call | tf_op jit(solution)/shard_map/moe/pallas_call | solution.py:484
  222.6 8.0 %flush.1 = (bf16[1024,768]{1,0:T(8,128)(2,1)}, bf16[1024,768]{1,0:T(8,128)(2,1)}, bf16[2,768,3072]{2,1,0:T(8,128)(2,1)}, bf16[2,3072,768]{2,1,0:T(8,128)(2,1)}, f32[64,768]{1,0:T(8,128)}, /*index=5*/f32[1,1]{1,0:T(1,128)}) custom-call(bf16[1024,768]{1,0:T(8,128)(2,1)S(1)} %get-tuple-element.18.y, bf16[1024,768]{1,0:T(8,128)(2,1)S(1)} %get-tuple-element.19.gx, ...), custom_call_target="tpu_custom_call" | custom-call | tf_op jit(solution)/shard_map/flush/pallas_call | solution.py:509

commit v5 on v4

--- a/solution.py
+++ b/solution.py
@@ -432,11 +432,13 @@
     def _(p):
         remote(all_s, all_in.at[mine], all_ss, all_rs, peer(p)).start()
     add_g(last, 0)
-    add_g(last, 1)
-
-    @pl.loop(0, stages)
+    await_group(lambda b: g_in.at[last, b], g_rs.at[last * stages + 1], 1)
+    end = group(1)
+    g_end = g_in[last, pl.ds(end * GROUP, GROUP)].reshape(rows, hidden)
+
+    @pl.loop(0, stages, unroll=2)
     def _(c):
-        gx_out[span(c), :] = big[span(c), :].astype(BF16)
+        gx_out[span(c), :] = (big[span(c), :] + dot(pick[span(c), span(end)], g_end)).astype(BF16)
     gathered = remote(all_in.at[some], all_in.at[some], all_ss, all_rs, me)
     gathered.wait_recv()
     for c in range(half):

time: 231 us -> 231 us (level)
  no operation moved by 1% of the time
where the time goes in v5:
time: 231 us
  Pallas kernels  230 us (100%)
    pallas_call x1, Pallas kernels, device_step(): pl.pallas_call(functools.partial(moe_kernel, n, loss_scale), out_shape=[f...  222 us
    pallas_call x1, Pallas kernels, device_step(): pl.pallas_call(flush_kernel, out_shape=[jax.ShapeDtypeStruct(v.shape, v.d...  8.03 us

profile of v5, /device:TPU:0, one launch (start us, length us, event | category | flops | bytes accessed | tf_op | source)
XLA Modules:
  0.0 230.6 jit_solution(9921619967647246294)
XLA Ops:
  0.6 221.9 %moe.1 = (bf16[1024,768]{1,0:T(8,128)(2,1)S(1)}, bf16[1024,768]{1,0:T(8,128)(2,1)S(1)}, bf16[2,768,3072]{2,1,0:T(8,128)(2,1)S(1)}, bf16[2,3072,768]{2,1,0:T(8,12...) custom-call(s32[2,1024]{1,0:T(2,128)} %picks.1, ...), custom_call_target="tpu_custom_call" | custom-call | tf_op jit(solution)/shard_map/moe/pallas_call | solution.py:486
  222.6 8.0 %flush.1 = (bf16[1024,768]{1,0:T(8,128)(2,1)}, bf16[1024,768]{1,0:T(8,128)(2,1)}, bf16[2,768,3072]{2,1,0:T(8,128)(2,1)}, bf16[2,3072,768]{2,1,0:T(8,128)(2,1)}, f32[64,768]{1,0:T(8,128)}, /*index=5*/f32[1,1]{1,0:T(1,128)}) custom-call(bf16[1024,768]{1,0:T(8,128)(2,1)S(1)} %get-tuple-element.18.y, bf16[1024,768]{1,0:T(8,128)(2,1)S(1)} %get-tuple-element.19.gx, ...), custom_call_target="tpu_custom_call" | custom-call | tf_op jit(solution)/shard_map/flush/pallas_call | solution.py:511
